TPU v7x, 32 devices: a whole 2x2x4 slice. The times are simulated.
32 devices in a mesh: row: 2 (over x), col: 4 (over y, core), layer: 4 (over z).
Axes of the slice: x: 2, y: 2, z: 4, core: 2. Of those that a mesh axis runs over, the one named last changes fastest.
Arguments:
- panel: float32 [1024, 8192], P('layer', ('col', 'row')), may hold values from -0.75 to 0.75
- c_in: float32 [4, 2, 1024, 8192], P('layer', 'row', None, 'col'), may hold values from -1.5 to 1.5
Outputs:
- updated: float32 [4, 2, 1024, 8192], P('layer', 'row', None, 'col')
All inputs are finite; a program needn't handle non-finite values.
Results may differ from a plain program's by a relative error of at most 0.000062.
Values sent between devices are 32-bit elements; how exact they have to be, the bound alone decides.
No kernel may reach another device: no remote copies, remote signals or barrier semaphores. Data moves between devices by JAX's collectives and lax.ppermute only.
A program may use at most 128 MiB of HBM per device.

v0:
```python
import jax
import jax.numpy as jnp
from jax import lax
from jax.sharding import PartitionSpec as P


def product(left, right):
    return lax.dot_general(
        left,
        right,
        (((0,), (0,)), ((), ())),
        precision=lax.Precision.HIGHEST,
        preferred_element_type=jnp.float32,
    )


def on_device(panel, c_in):
    narrow = c_in.shape[2]
    spread = lax.all_gather(panel, "col", axis=1, tiled=True)
    local = lax.all_gather(panel, "row", axis=1, tiled=True)
    pairs = (spread, local)
    groups = pairs[0].shape[1] // narrow
    columns_here = pairs[1].shape[1]
    spread, local = pairs
    tile = product(spread, local)
    tile = tile.reshape(groups, 1, narrow, columns_here)
    summed = lax.psum_scatter(tile, "layer", scatter_dimension=0, tiled=True)
    return c_in + summed


def solution(mesh):
    placed = (P("layer", ("col", "row")), P("layer", "row", None, "col"))
    return jax.shard_map(
        on_device,
        mesh=mesh,
        in_specs=placed,
        out_specs=P("layer", "row", None, "col"),
        check_vma=False,
    )
```

profile of v0, /device:TPU:0, one launch (start us, length us, event | category | flops | bytes accessed | tf_op | source)
XLA Modules:
  0.0 683.8 jit_solution(14845366187475919267)
XLA Ops:
  6.5 0.0 all-gather.5.cloned.1.call-start
  6.5 0.7 all-gather.5.cloned.1.call-update
  7.3 0.0 all-gather.3.cloned.1.call-start
  7.3 0.7 all-gather.3.cloned.1.call-update
  8.0 0.0 reduce-scatter.2.cloned.1.call-start
  8.1 36.7 %all-gather.5.cloned.1.call-done = f32[256,2048]{1,0:T(8,128)} async-done(((f32[256,1024]{1,0:T(8,128)}), f32[256,2048]{1,0:T(8,128)}) %all-gather.5.cloned.1.call-update) | async-done | bytes 2097168 | tf_op jit(solution)/shard_map/all_gather | solution.py:20
  44.7 36.1 %all-gather.3.cloned.1.call-done = f32[256,4096]{1,0:T(8,128)} async-done(((f32[256,1024]{1,0:T(8,128)}), f32[256,4096]{1,0:T(8,128)}) %all-gather.3.cloned.1.call-update) | async-done | bytes 4194320 | tf_op jit(solution)/shard_map/all_gather | solution.py:19
  80.8 32.3 %fusion = f32[4096,2048]{1,0:T(8,128)} fusion(f32[256,4096]{1,0:T(8,128)} %all-gather.3.cloned.1.call-done, f32[256,2048]{1,0:T(8,128)} %all-gather.5.cloned.1.call-done), kind=kOutput, calls=%fused_computation | convolution fusion | flops 25769803776 | bytes 39845888 | tf_op jit(solution)/shard_map/dot_general | solution.py:8
  113.1 0.0 reduce-scatter.2.cloned.1.call-update
  113.1 552.3 %reduce-scatter.2.cloned.1.call-done = f32[1,1,1024,2048]{3,2,1,0:T(8,128)} async-done(((f32[4,1,1024,2048]{3,2,1,0:T(8,128)}), f32[1,1,1024,2048]{3,2,1,0:T(8,128)}) %reduce-scatter.2.cloned.1.call-update) | async-done | bytes 8388624 | tf_op jit(solution)/shard_map/reduce_scatter | solution.py:27
  665.4 11.9 %add.5 = f32[1,1,1024,2048]{3,2,1,0:T(8,128)} add(f32[1,1,1024,2048]{3,2,1,0:T(8,128)} %param.3, f32[1,1,1024,2048]{3,2,1,0:T(8,128)} %reduce-scatter.2.cloned.1.call-done) | non-fusion elementwise | flops 2097152 | bytes 25165824 | tf_op jit(solution)/shard_map/add | solution.py:28
Async XLA Ops:
  6.5 38.2 %all-gather.5.cloned.1.call-start = ((), (), s32[]{:S(2)}) async-start(), calls=%async_computation.2 | async-start | bytes 3145728 | tf_op jit(solution)/shard_map/all_gather | solution.py:20
  7.3 73.5 %all-gather.3.cloned.1.call-start = ((), (), s32[]{:S(2)}) async-start(), calls=%async_computation.1 | async-start | bytes 5242880 | tf_op jit(solution)/shard_map/all_gather | solution.py:19
  8.0 657.4 %reduce-scatter.2.cloned.1.call-start = ((), (), s32[]{:S(2)}) async-start(), calls=%async_computation.3 | async-start | bytes 41943040 | tf_op jit(solution)/shard_map/reduce_scatter | solution.py:27
Sparse Core Ops, SparseCore 0:
  8.9 35.8 all-gather.4
  46.3 34.4 all-gather.2
  113.2 552.1 reduce-scatter.1
where the time goes:
time: 684 us
  waiting for transfers between devices  626 us (92%)
  matrix products  32.3 us (5%)
  between operations  13.1 us (2%)
  other arithmetic  11.9 us (2%)
    reduce_scatter x1, waiting for transfers between devices, on_device(): summed = lax.psum_scatter(tile, 'layer', scatter_dimension=0, tiled=True)  552 us
    all_gather x1, waiting for transfers between devices, on_device(): local = lax.all_gather(panel, 'row', axis=1, tiled=True)  36.7 us
    all_gather x1, waiting for transfers between devices, on_device(): spread = lax.all_gather(panel, 'col', axis=1, tiled=True)  36.1 us
    dot_general x1, matrix products, product(): lax.dot_general(left, right, (((0,), (0,)), ((), ())), precision=lax.Prec...  32.3 us
  transfers between devices with their start and end apart: 3, of which 3 were waited for; matrix products, arithmetic and copies ran while one was open for 0% of the time, Pallas kernels for 0%

commit v1 on v0

v1 whole, which is shorter than its diff:
```python
import functools

import jax
import jax.numpy as jnp
from jax import lax
from jax.experimental import pallas as pl
from jax.experimental.pallas import tpu as pltpu
from jax.sharding import PartitionSpec as P

AXES = ("row", "col", "layer")
F32, BF16 = jnp.float32, jnp.bfloat16
VMEM = pl.BlockSpec(memory_space=pltpu.VMEM)
SMEM = pl.BlockSpec(memory_space=pltpu.SMEM)
ANY = pl.BlockSpec(memory_space=pl.ANY)


def split(x):
    high = x.astype(BF16)
    return high, (x - high.astype(F32)).astype(BF16)


def stacked_left(x):
    high, low = split(x)
    return jnp.concatenate([high, high, low], 0)


def stacked_right(x):
    high, low = split(x)
    return jnp.concatenate([high, low, high], 0)


def dot(left, right):
    return lax.dot_general(left, right, (((0,), (0,)), ((), ())), preferred_element_type=F32)


def params(mib):
    return pltpu.CompilerParams(vmem_limit_bytes=mib << 20, has_side_effects=True)


def cost(flops):
    return pl.CostEstimate(flops=flops, bytes_accessed=1 << 20, transcendentals=0)


def call(kernel, args, outs, aliases=None, scratch=(), flops=1 << 20, mib=40):
    return pl.pallas_call(
        kernel,
        in_specs=[spec for _, spec in args],
        out_specs=[spec for _, spec in outs],
        out_shape=[shape for shape, _ in outs],
        input_output_aliases=aliases or {},
        scratch_shapes=scratch,
        compiler_params=params(mib),
        cost_estimate=cost(flops),
    )(*(a for a, _ in args))


def load_acc(flags, c, own, other, sems):
    width = own.shape[1]
    row = flags[0]
    copies = [
        pltpu.make_async_copy(c.at[:, pl.ds(pl.multiple_of(row * width, width), width)], own, sems.at[0]),
        pltpu.make_async_copy(c.at[:, pl.ds(pl.multiple_of((1 - row) * width, width), width)], other, sems.at[1]),
    ]
    for copy in copies:
        copy.start()
    for copy in copies:
        copy.wait()


def choose(which, flags, *refs):
    flag = flags[which] == 1
    n = len(refs) // 3
    for a, b, out in zip(refs[:n], refs[n : 2 * n], refs[2 * n :], strict=True):

        @pl.when(flag)
        def _():
            out[...] = a[...]

        @pl.when(jnp.logical_not(flag))
        def _():
            out[...] = b[...]


def select(which, flags, firsts, seconds):
    shapes = [(pltpu.VMEM(a.shape, F32), VMEM) for a in firsts]
    args = [(flags, SMEM)] + [(a, VMEM) for a in (*firsts, *seconds)]
    return call(functools.partial(choose, which), args, shapes, mib=8)


def pick(flag, a, b):
    return lax.select(jnp.full(a.shape, flag), a, b)


class Pieces:
    def __init__(self, firsts, which=None, seconds=()):
        self.firsts, self.which, self.seconds = tuple(firsts), which, tuple(seconds)

    @property
    def arrays(self):
        return self.firsts + self.seconds

    def reader(self, flags, refs):
        firsts, seconds = refs[: len(self.firsts)], refs[len(self.firsts) :]

        def read(columns=slice(None)):
            def rows(group):
                parts = [r[:, columns] for r in group]
                return parts[0] if len(parts) == 1 else jnp.concatenate(parts, 0)

            if self.which is None:
                return rows(firsts)
            return pick(flags[self.which] == 1, rows(firsts), rows(seconds))

        return read


def accumulate(flags, terms, accs, tile=256):
    operands = [p for left, rights in terms for p in (left, *rights)]
    n_acc = len(accs)

    def kernel(flag_ref, *refs):
        at = 0
        readers = []
        for p in operands:
            readers.append(p.reader(flag_ref, refs[at : at + len(p.arrays)]))
            at += len(p.arrays)
        olds, news = refs[at : at + n_acc], refs[at + n_acc :]
        at = 0
        for left, rights in terms:
            stack = stacked_left(readers[at]())
            for i in range(n_acc):
                for j in range(0, olds[i].shape[1], tile):
                    cols = slice(j, j + tile)
                    base = olds[i] if at == 0 else news[i]
                    news[i][:, cols] = base[:, cols] + dot(stack, stacked_right(readers[at + 1 + i](cols)))
            at += 1 + n_acc

    arrays = [a for p in operands for a in p.arrays]
    args = [(flags, SMEM)] + [(a, VMEM) for a in arrays] + [(a, VMEM) for a in accs]
    outs = [(pltpu.VMEM(a.shape, F32), VMEM) for a in accs]
    first = 1 + len(arrays)
    flops = sum(6 * l.arrays[0].shape[0] * a.shape[0] * a.shape[1] for l, _ in terms for a in accs)
    return call(kernel, args, outs, {first + i: i for i in range(n_acc)}, flops=flops)


def finish(flags, terms, acc, half, shape, so_far=None, tile=256):
    operands = [p for left, right in terms for p in (left, right)]
    tiles = acc.shape[1] // tile

    def kernel(flag_ref, *refs):
        readers = []
        at = 0
        for p in operands:
            readers.append(p.reader(flag_ref, refs[at : at + len(p.arrays)]))
            at += len(p.arrays)
        old = refs[at]
        out, stack = refs[-2], refs[-1]
        j = pl.program_id(0)

        @pl.when(j == 0)
        def _():
            rows = 0
            for i in range(0, len(readers), 2):
                left = stacked_left(readers[i]())
                stack[rows : rows + left.shape[0]] = left
                rows += left.shape[0]

        cols = pl.ds(pl.multiple_of(j * tile, tile), tile)
        rights = [stacked_right(readers[i](cols)) for i in range(1, len(readers), 2)]
        right = rights[0] if len(rights) == 1 else jnp.concatenate(rights, 0)
        out[...] = old[:, cols] + dot(stack[...], right)

    arrays = [a for p in operands for a in p.arrays]
    args = arrays + [acc] + ([] if so_far is None else [so_far])
    specs = [VMEM] * (len(arrays) + 1) + ([] if so_far is None else [ANY])
    depth = sum(3 * sum(a.shape[0] for a in left.firsts) for left, _ in terms)
    return pl.pallas_call(
        kernel,
        grid_spec=pltpu.PrefetchScalarGridSpec(
            num_scalar_prefetch=1,
            grid=(tiles,),
            in_specs=specs,
            out_specs=pl.BlockSpec((acc.shape[0], tile), lambda j, flag_ref: (0, flag_ref[half] * tiles + j)),
            scratch_shapes=[pltpu.VMEM((depth, acc.shape[0]), BF16)],
        ),
        out_shape=jax.ShapeDtypeStruct(shape, F32),
        input_output_aliases={} if so_far is None else {len(args): 0},
        compiler_params=params(40),
        cost_estimate=cost(2 * depth * acc.shape[0] * acc.shape[1]),
    )(flags, *args)


def paired(mesh, panel, c_in):
    n_row, n_col, n_layer = (mesh.shape[a] for a in AXES)

    def send(x, to):
        pairs = []
        for r in range(n_row):
            for c in range(n_col):
                for l in range(n_layer):
                    target = to(r, c, l)
                    if target is not None:
                        a, b, d = target
                        pairs.append(((r * n_col + c) * n_layer + l, (a * n_col + b) * n_layer + d))
        return lax.ppermute(x, AXES, pairs)

    inner = lambda l: l in (1, 2)
    near = lambda r, c, l: (r, c, l ^ 1)
    outward = lambda r, c, l: (r, c, l ^ 1) if inner(l) else None
    middle = lambda r, c, l: (r, c, 3 - l) if inner(l) else None
    swap = lambda r, c, l: (1 - r, c, l)
    swap_ends = lambda r, c, l: None if inner(l) else (1 - r, c, l)
    across = lambda r, c, l: (r, c ^ 2, l) if c == l else None
    beside = lambda r, c, l: (r, c ^ 1, l) if c in (l, l ^ 2) else None

    row, col, layer = (lax.axis_index(a) for a in AXES)
    is_inner = (layer == 1) | (layer == 2)
    is_source = col == layer
    is_holder = is_source | (col == layer ^ 2)
    flags = jnp.stack([row, 1 - row, is_inner, is_source, is_holder]).astype(jnp.int32)
    INNER, SOURCE, HOLDER = 2, 3, 4

    depth, width = panel.shape
    half = depth // 2
    c_flat = c_in.reshape(c_in.shape[2:])
    p0a, p0b = panel[:half], panel[half:]

    a1a = send(p0a, near)
    x1 = send(panel, swap)
    b1a = send(p0a, middle)
    y0 = send(panel, across)
    a1b = send(p0b, near)
    b1b = send(p0b, middle)

    acc = [(pltpu.VMEM((c_flat.shape[0], width), F32), VMEM)] * 2
    own, other = call(load_acc, [(flags, SMEM), (c_flat, ANY)], acc, scratch=[pltpu.SemaphoreType.DMA((2,))], mib=20)

    a2a = send(b1a, outward)
    x2a = send(a1a, swap)
    b2a = send(a1a, middle)
    y1a = send(a1a, across)
    (m_0,) = select(SOURCE, flags, [panel], [y0])
    d0 = send(m_0, beside)

    a2b = send(b1b, outward)
    x2b = send(a1b, swap)
    b2b = send(a1b, middle)
    y1b = send(a1b, across)

    l0 = Pieces([m_0], HOLDER, [d0])
    own, other = accumulate(flags, [(l0, [Pieces([panel]), Pieces([x1])])], [own, other])

    a3a = send(b2a, outward)
    (s3a,) = select(INNER, flags, [b2a], [a2a])
    x3a = send(s3a, swap)
    m_1a, m_1b = select(SOURCE, flags, [a1a, a1b], [y1a, y1b])
    d1a = send(m_1a, beside)
    d1b = send(m_1b, beside)

    a3b = send(b2b, outward)
    s3b, p2a, p2b = select(INNER, flags, [b2b, b1a, b1b], [a2b, a2a, a2b])
    x3b = send(s3b, swap)
    y2a = send(p2a, across)
    y2b = send(p2b, across)
    b3 = send(x1, middle)

    l1 = Pieces([m_1a, m_1b], HOLDER, [d1a, d1b])
    own, other = accumulate(flags, [(l1, [Pieces([a1a, a1b]), Pieces([x2a, x2b])])], [own, other])

    a4 = send(x3a, outward)
    (p3a,) = select(INNER, flags, [b2a], [a3a])
    y3a = send(p3a, across)
    m_2a, m_2b = select(SOURCE, flags, [p2a, p2b], [y2a, y2b])
    d2a = send(m_2a, beside)
    d2b = send(m_2b, beside)

    x4 = send(a3b, swap_ends)
    (p3b,) = select(INNER, flags, [b2b], [a3b])
    y3b = send(p3b, across)
    (m_3a,) = select(SOURCE, flags, [p3a], [y3a])
    d3a = send(m_3a, beside)

    l2 = Pieces([m_2a, m_2b], HOLDER, [d2a, d2b])
    q2 = Pieces([b3], INNER, [x3a, x3b])
    q2 = Pieces([b3[:half], b3[half:]], INNER, [x3a, x3b]) if False else q2
    own, other = accumulate(flags, [(l2, [Pieces([p2a, p2b]), q2])], [own, other])

    (m_3b,) = select(SOURCE, flags, [p3b], [y3b])
    d3b = send(m_3b, beside)
    l3 = Pieces([m_3a, m_3b], HOLDER, [d3a, d3b])
    out = finish(flags, [(l3, Pieces([p3a, p3b]))], own, 0, c_flat.shape)
    q3 = Pieces([x3a, x3b], INNER, [a4, x4])
    out = finish(flags, [(l3, q3)], other, 1, c_flat.shape, out)
    return out.reshape(c_in.shape)


def gathered(panel, c_in):
    rows_here, width = c_in.shape[0], panel.shape[1]
    own = lax.all_gather(panel, "layer", axis=0, tiled=True)
    right = lax.all_gather(own, "row", axis=1, tiled=True)
    columns = lax.all_gather(own, "col", axis=0)
    mine = lax.dynamic_slice_in_dim(columns, lax.axis_index("layer") * rows_here, rows_here, 0)
    left = jnp.moveaxis(mine, 0, 1).reshape(own.shape[0], rows_here * width)
    tile = lax.dot_general(
        left, right, (((0,), (0,)), ((), ())), precision=lax.Precision.HIGHEST, preferred_element_type=F32
    )
    return c_in + tile.reshape(c_in.shape)


def solution(mesh):
    placed = (P("layer", ("col", "row")), P("layer", "row", None, "col"))
    fits = tuple(mesh.shape[a] for a in AXES) == (2, 4, 4)

    def on_device(panel, c_in):
        if not fits:
            return gathered(panel, c_in)
        return paired(mesh, panel, c_in)

    return jax.shard_map(
        on_device,
        mesh=mesh,
        in_specs=placed,
        out_specs=P("layer", "row", None, "col"),
        check_vma=False,
    )
```

time: 684 us -> 155 us (0.23)
  the two profiles are of different devices: /device:TPU:0 before, /device:TPU:20 now
where the time goes in v1:
time: 155 us; the launch traced here: 154 us
  starting transfers between devices  59.6 us (38%)
  waiting for transfers between devices  43.4 us (28%)
  Pallas kernels  35.9 us (23%)
  local copies, waits for them, and re-layouts  14.5 us (9%)
    ppermute x32, starting transfers between devices, send(): return lax.ppermute(x, AXES, pairs)  59.6 us
    ppermute x32, waiting for transfers between devices, send(): return lax.ppermute(x, AXES, pairs)  43.4 us
    pallas_call x13, Pallas kernels, call(): pl.pallas_call(kernel, in_specs=[spec for _, spec in args], out_specs=[sp...  25.2 us
    unnamed x44, local copies, waits for them, and re-layouts  13 us
    pallas_call x2, Pallas kernels, finish(): pl.pallas_call(kernel, grid_spec=pltpu.PrefetchScalarGridSpec(num_scalar_...  10.7 us
  transfers between devices with their start and end apart: 32, of which 9 were waited for; matrix products, arithmetic and copies ran while one was open for 0% of the time, Pallas kernels for 20%

profile of v1, /device:TPU:20, one launch (start us, length us, event | category | flops | bytes accessed | tf_op | source)
XLA Modules:
  0.0 153.8 jit_solution(14300537472337272345)
XLA Ops:
  0.0 1.4 fusion
  1.4 1.6 %collective-permute-start = (f32[128,1024]{1,0:T(8,128)S(1)}, f32[128,1024]{1,0:T(8,128)S(1)}, u32[]{:S(2)}, u32[]{:S(2)}) collective-permute-start(f32[128,1024]{1,0:T(8,128)S(1)} %get-tuple-element.36), channel_id=1, source_target_pairs={{0,1},{1,0},{2,3},{3,2},{4,5},{5,4},{6,7},{7,6},{8,9},{9,8},{10,11... | collective-permute-start | bytes 1572872 | tf_op jit(solution)/shard_map/ppermute | solution.py:205
  3.5 2.3 %collective-permute-start.10 = (f32[128,1024]{1,0:T(8,128)S(1)}, f32[128,1024]{1,0:T(8,128)S(1)}, u32[]{:S(2)}, u32[]{:S(2)}) collective-permute-start(f32[128,1024]{1,0:T(8,128)S(1)} %get-tuple-element.36), channel_id=1, source_target_pairs={{1,2},{2,1},{5,6},{6,5},{9,10},{10,9},{13,14},{14,13},{17,18},{18,... | collective-permute-start | bytes 1572872 | tf_op jit(solution)/shard_map/ppermute | solution.py:205
  5.8 3.5 %collective-permute-start.13 = (f32[128,1024]{1,0:T(8,128)S(1)}, f32[128,1024]{1,0:T(8,128)S(1)}, u32[]{:S(2)}, u32[]{:S(2)}) collective-permute-start(f32[128,1024]{1,0:T(8,128)S(1)} %get-tuple-element.35), channel_id=1, source_target_pairs={{1,2},{2,1},{5,6},{6,5},{9,10},{10,9},{13,14},{14,13},{17,18},{18,... | collective-permute-start | bytes 1572872 | tf_op jit(solution)/shard_map/ppermute | solution.py:205
  9.3 6.9 %collective-permute-done.refs_0_.refs_4_ = f32[128,1024]{1,0:T(8,128)S(1)} collective-permute-done((f32[128,1024]{1,0:T(8,128)S(1)}, f32[128,1024]{1,0:T(8,128)S(1)}, u32[]{:S(2)}, u32[]{:S(2)}) %collective-permute-start) | collective-permute-done | bytes 524320 | tf_op jit(solution)/shard_map/ppermute | solution.py:205
  16.3 2.4 %collective-permute-start.24 = (f32[128,1024]{1,0:T(8,128)S(1)}, f32[128,1024]{1,0:T(8,128)S(1)}, u32[]{:S(2)}, u32[]{:S(2)}) collective-permute-start(f32[128,1024]{1,0:T(8,128)S(1)} %collective-permute-done.refs_0_.refs_4_), channel_id=1, source_target_pairs={{0,8},{5,13},{10,2},{15,7},{16,24},{21,29},{26,18},{31,23}} | collective-permute-start | bytes 1572872 | tf_op jit(solution)/shard_map/ppermute | solution.py:205
  18.7 7.7 %collective-permute-done.4.refs_1_.refs_5_ = f32[128,1024]{1,0:T(8,128)S(1)} collective-permute-done((f32[128,1024]{1,0:T(8,128)S(1)}, f32[128,1024]{1,0:T(8,128)S(1)}, u32[]{:S(2)}, u32[]{:S(2)}) %collective-permute-start.4) | collective-permute-done | bytes 524320 | tf_op jit(solution)/shard_map/ppermute | solution.py:205
  26.4 2.4 %collective-permute-start.25 = (f32[128,1024]{1,0:T(8,128)S(1)}, f32[128,1024]{1,0:T(8,128)S(1)}, u32[]{:S(2)}, u32[]{:S(2)}) collective-permute-start(f32[128,1024]{1,0:T(8,128)S(1)} %collective-permute-done.4.refs_1_.refs_5_), channel_id=1, source_target_pairs={{0,8},{5,13},{10,2},{15,7},{16,24},{21,29},{26,18},{31,23}} | collective-permute-start | bytes 1572872 | tf_op jit(solution)/shard_map/ppermute | solution.py:205
  28.8 1.9 %collective-permute-start.5 = (f32[128,1024]{1,0:T(8,128)S(1)}, f32[128,1024]{1,0:T(8,128)}, u32[]{:S(2)}, u32[]{:S(2)}) collective-permute-start(f32[128,1024]{1,0:T(8,128)S(1)} %collective-permute-done.4.refs_1_.refs_5_), channel_id=1, source_target_pairs={{1,2},{2,1},{5,6},{6,5},{9,10},{10,9},{13,14},{14,13},{17,18},{18,... | collective-permute-start | bytes 1572872 | tf_op jit(solution)/shard_map/ppermute | solution.py:205
  30.7 2.3 %collective-permute-start.30 = (f32[256,1024]{1,0:T(8,128)}, f32[256,1024]{1,0:T(8,128)}, u32[]{:S(2)}, u32[]{:S(2)}) collective-permute-start(f32[256,1024]{1,0:T(8,128)} %refs_2_.1), channel_id=1, source_target_pairs={{0,8},{5,13},{10,2},{15,7},{16,24},{21,29},{26,18},{31,23}} | collective-permute-start | bytes 3145736 | tf_op jit(solution)/shard_map/ppermute | solution.py:205
  33.0 1.5 collective-permute-start.22
  35.3 1.3 collective-permute-start.11
  38.3 1.3 collective-permute-start.14
  40.4 1.4 collective-permute-done.5.refs_0_
  41.9 2.9 %collective-permute-start.1 = (f32[128,1024]{1,0:T(8,128)S(1)}, f32[128,1024]{1,0:T(8,128)S(1)}, u32[]{:S(2)}, u32[]{:S(2)}) collective-permute-start(f32[128,1024]{1,0:T(8,128)S(1)} %collective-permute-done.refs_0_.refs_4_), channel_id=1, source_target_pairs={{1,2},{2,1},{5,6},{6,5},{9,10},{10,9},{13,14},{14,13},{17,18},{18,... | collective-permute-start | bytes 1572872 | tf_op jit(solution)/shard_map/ppermute | solution.py:205
  44.8 4.1 %collective-permute-done.11.refs_1_.refs_4_ = f32[128,1024]{1,0:T(8,128)S(1)} collective-permute-done((f32[128,1024]{1,0:T(8,128)S(1)}, f32[128,1024]{1,0:T(8,128)S(1)}, u32[]{:S(2)}, u32[]{:S(2)}) %collective-permute-start.11) | collective-permute-done | bytes 524320 | tf_op jit(solution)/shard_map/ppermute | solution.py:205
  50.2 9.1 %collective-permute-done.14.refs_3_.refs_5_ = f32[128,1024]{1,0:T(8,128)S(1)} collective-permute-done((f32[128,1024]{1,0:T(8,128)S(1)}, f32[128,1024]{1,0:T(8,128)S(1)}, u32[]{:S(2)}, u32[]{:S(2)}) %collective-permute-start.14) | collective-permute-done | bytes 524320 | tf_op jit(solution)/shard_map/ppermute | solution.py:205
  60.1 5.2 %collective-permute-start.6 = (f32[128,1024]{1,0:T(8,128)}, f32[128,1024]{1,0:T(8,128)}, u32[]{:S(2)}, u32[]{:S(2)}) collective-permute-start(f32[128,1024]{1,0:T(8,128)} %collective-permute-done.5.refs_0_), channel_id=1, source_target_pairs={{1,0},{2,3},{5,4},{6,7},{9,8},{10,11},{13,12},{14,15},{17,16},{18,... | collective-permute-start | bytes 1572872 | tf_op jit(solution)/shard_map/ppermute | solution.py:205
  65.3 2.1 %collective-permute-start.2 = (f32[128,1024]{1,0:T(8,128)S(1)}, f32[128,1024]{1,0:T(8,128)}, u32[]{:S(2)}, u32[]{:S(2)}) collective-permute-start(f32[128,1024]{1,0:T(8,128)S(1)} %collective-permute-done.1.refs_0_), channel_id=1, source_target_pairs={{1,0},{2,3},{5,4},{6,7},{9,8},{10,11},{13,12},{14,15},{17,16},{18,... | collective-permute-start | bytes 1572872 | tf_op jit(solution)/shard_map/ppermute | solution.py:205
  67.5 1.0 copy-done.7
  68.5 1.0 copy-done.9
  70.2 1.3 copy-done.2
  74.7 1.2 shard_map.33
  76.5 1.3 collective-permute-start.26
  77.9 1.3 collective-permute-start.27
  79.2 1.6 %collective-permute-start.18 = (f32[128,1024]{1,0:T(8,128)S(1)}, f32[128,1024]{1,0:T(8,128)S(1)}, u32[]{:S(2)}, u32[]{:S(2)}) collective-permute-start(f32[128,1024]{1,0:T(8,128)S(1)} %get-tuple-element.21.refs_0_.refs_4_), channel_id=1, source_target_pairs={{0,8},{5,13},{10,2},{15,7},{16,24},{21,29},{26,18},{31,23}} | collective-permute-start | bytes 1572872 | tf_op jit(solution)/shard_map/ppermute | solution.py:205
  80.8 5.9 %collective-permute-done.2.refs_1_ = f32[128,1024]{1,0:T(8,128)} collective-permute-done((f32[128,1024]{1,0:T(8,128)S(1)}, f32[128,1024]{1,0:T(8,128)}, u32[]{:S(2)}, u32[]{:S(2)}) %collective-permute-start.2) | collective-permute-done | bytes 524320 | tf_op jit(solution)/shard_map/ppermute | solution.py:205
  86.6 1.7 %collective-permute-start.19 = (f32[128,1024]{1,0:T(8,128)S(1)}, f32[128,1024]{1,0:T(8,128)S(1)}, u32[]{:S(2)}, u32[]{:S(2)}) collective-permute-start(f32[128,1024]{1,0:T(8,128)S(1)} %get-tuple-element.22.refs_1_.refs_5_), channel_id=1, source_target_pairs={{0,8},{5,13},{10,2},{15,7},{16,24},{21,29},{26,18},{31,23}} | collective-permute-start | bytes 1572872 | tf_op jit(solution)/shard_map/ppermute | solution.py:205
  88.4 1.3 shard_map.36.refs_0_
  89.7 1.3 shard_map.30.refs_0_.refs_5_
  91.0 1.1 shard_map.28.refs_0_.refs_4_
  92.7 1.3 collective-permute-start.7
  94.0 1.4 collective-permute-start.31
  95.4 1.3 collective-permute-start.3
  96.7 1.9 %collective-permute-start.23 = (f32[256,1024]{1,0:T(8,128)}, f32[256,1024]{1,0:T(8,128)S(1)}, u32[]{:S(2)}, u32[]{:S(2)}) collective-permute-start(f32[256,1024]{1,0:T(8,128)} %collective-permute-done.22.refs_3_), channel_id=1, source_target_pairs={{1,2},{2,1},{5,6},{6,5},{9,10},{10,9},{13,14},{14,13},{17,18},{18,... | collective-permute-start | bytes 3145736 | tf_op jit(solution)/shard_map/ppermute | solution.py:205
  99.9 4.3 %collective-permute-done.15.refs_8_.refs_5_ = f32[128,1024]{1,0:T(8,128)S(1)} collective-permute-done((f32[128,1024]{1,0:T(8,128)S(1)}, f32[128,1024]{1,0:T(8,128)S(1)}, u32[]{:S(2)}, u32[]{:S(2)}) %collective-permute-start.15) | collective-permute-done | bytes 524320 | tf_op jit(solution)/shard_map/ppermute | solution.py:205
  104.8 1.3 collective-permute-start.20
  106.3 1.3 collective-permute-start.21
  107.6 2.6 %shard_map.37 = (f32[1024,1024]{1,0:T(8,128)S(1)}, f32[1024,1024]{1,0:T(8,128)S(1)}) custom-call(s32[5]{0:T(128)S(1)} %stack.35.flags.flag_ref, f32[1024,2048]{1,0:T(8,128)S(1)} %bitcast.9), custom_call_target="tpu_custom_call" | custom-call | flops 1048576 | bytes 1048576 | tf_op jit(solution)/shard_map/pallas_call | solution.py:45
  111.4 3.8 %collective-permute-done.12.refs_7_.refs_4_ = f32[128,1024]{1,0:T(8,128)S(1)} collective-permute-done((f32[128,1024]{1,0:T(8,128)S(1)}, f32[128,1024]{1,0:T(8,128)S(1)}, u32[]{:S(2)}, u32[]{:S(2)}) %collective-permute-start.12) | collective-permute-done | bytes 524320 | tf_op jit(solution)/shard_map/ppermute | solution.py:205
  115.9 8.0 %collective-permute-start.16 = (f32[128,1024]{1,0:T(8,128)S(1)}, f32[128,1024]{1,0:T(8,128)}, u32[]{:S(2)}, u32[]{:S(2)}) collective-permute-start(f32[128,1024]{1,0:T(8,128)S(1)} %collective-permute-done.12.refs_7_.refs_4_), channel_id=1, source_target_pairs={{1,0},{2,3},{5,4},{6,7},{9,8},{10,11},{13,12},{14,15},{17,16},{18,... | collective-permute-start | bytes 1572872 | tf_op jit(solution)/shard_map/ppermute | solution.py:205
  124.7 1.3 collective-permute-start.9
  126.8 1.5 collective-permute-start.8
  128.3 5.2 %shard_map.38 = (f32[1024,1024]{1,0:T(8,128)S(1)}, f32[1024,1024]{1,0:T(8,128)S(1)}) custom-call(s32[5]{0:T(128)S(1)} %stack.35.flags.flag_ref, f32[256,1024]{1,0:T(8,128)S(1)} %shard_map.36.refs_0_, f32[256,1024]{1,0:T(8,128)S(1)} %collective-permute-done.31.refs_1_, f32[256,1024]{1,0:T(8,128)S(1)} %copy-done, ...), custom_call_target="tpu_custom_call", output_to_operand_aliasing={{0}: (5, {}), {1}: (6, {})} | custom-call | flops 3221225472 | bytes 1048576 | tf_op jit(solution)/shard_map/pallas_call | solution.py:45
  133.5 5.1 %shard_map.39 = (f32[1024,1024]{1,0:T(8,128)S(1)}, f32[1024,1024]{1,0:T(8,128)S(1)}) custom-call(s32[5]{0:T(128)S(1)} %stack.35.flags.flag_ref, f32[128,1024]{1,0:T(8,128)S(1)} %get-tuple-element.25.refs_0_, f32[128,1024]{1,0:T(8,128)S(1)} %get-tuple-element.26.refs_1_, ...), custom_call_target="tpu_custom_call", output_to_operand_aliasing={{0}: (9, {}), {1}: (10, {})} | custom-call | flops 1610612736 | bytes 1048576 | tf_op jit(solution)/shard_map/pallas_call | solution.py:45
  138.7 4.5 %shard_map.40 = (f32[1024,1024]{1,0:T(8,128)S(1)}, f32[1024,1024]{1,0:T(8,128)S(1)}) custom-call(s32[5]{0:T(128)S(1)} %stack.35.flags.flag_ref, f32[128,1024]{1,0:T(8,128)S(1)} %get-tuple-element.23.refs_0_, f32[128,1024]{1,0:T(8,128)S(1)} %copy-done.15, f32[128,1024]{1,0:T(8,128)S(1)} %copy-done.17, ...), custom_call_target="tpu_custom_call", output_to_operand_aliasing={{0}: (10, {}), {1}: (11, {})} | custom-call | flops 1610612736 | bytes 1048576 | tf_op jit(solution)/shard_map/pallas_call | solution.py:45
  143.2 4.8 %shard_map.41.refs_9_ = f32[1024,2048]{1,0:T(8,128)} custom-call(s32[5]{0:T(128)S(1)} %stack.35.flags.flag_ref, f32[128,1024]{1,0:T(8,128)S(1)} %shard_map.29.refs_0_, f32[128,1024]{1,0:T(8,128)S(1)} %shard_map.31.refs_1_, f32[128,1024]{1,0:T(8,128)S(1)} %collective-permute-done.8.refs_2_, f32[128,1024]{1,0:T(8,128)S(1)} %collective-permute-done.9.refs_3_, ...), custom_call_target="tpu_custom_call" | custom-call | flops 1610612736 | bytes 1048576 | tf_op jit(solution)/shard_map/pallas_call | solution.py:177
  148.0 5.8 %shard_map.42 = f32[1024,2048]{1,0:T(8,128)} custom-call(s32[5]{0:T(128)S(1)} %stack.35.flags.flag_ref, f32[128,1024]{1,0:T(8,128)S(1)} %shard_map.29.refs_0_, f32[128,1024]{1,0:T(8,128)S(1)} %shard_map.31.refs_1_, f32[128,1024]{1,0:T(8,128)S(1)} %collective-permute-done.8.refs_2_, ...), custom_call_target="tpu_custom_call", output_to_operand_aliasing={{}: (10, {})} | custom-call | flops 1610612736 | bytes 1048576 | tf_op jit(solution)/shard_map/pallas_call | solution.py:177
  (78 shorter events, 16.3 us)
Async XLA Ops:
  0.0 88.4 %copy-start = (f32[256,1024]{1,0:T(8,128)S(1)}, f32[256,1024]{1,0:T(8,128)}, u32[]{:S(2)}) copy-start(f32[256,1024]{1,0:T(8,128)} %refs_2_.1) | copy-start | bytes 3145732
  1.4 14.9 %collective-permute-start = (f32[128,1024]{1,0:T(8,128)S(1)}, f32[128,1024]{1,0:T(8,128)S(1)}, u32[]{:S(2)}, u32[]{:S(2)}) collective-permute-start(f32[128,1024]{1,0:T(8,128)S(1)} %get-tuple-element.36), channel_id=1, source_target_pairs={{0,1},{1,0},{2,3},{3,2},{4,5},{5,4},{6,7},{7,6},{8,9},{9,8},{10,11... | collective-permute-start | bytes 1572872 | tf_op jit(solution)/shard_map/ppermute | solution.py:205
  3.0 23.3 %collective-permute-start.4 = (f32[128,1024]{1,0:T(8,128)S(1)}, f32[128,1024]{1,0:T(8,128)S(1)}, u32[]{:S(2)}, u32[]{:S(2)}) collective-permute-start(f32[128,1024]{1,0:T(8,128)S(1)} %get-tuple-element.35), channel_id=1, source_target_pairs={{0,1},{1,0},{2,3},{3,2},{4,5},{5,4},{6,7},{7,6},{8,9},{9,8},{10,11... | collective-permute-start | bytes 1572872 | tf_op jit(solution)/shard_map/ppermute | solution.py:205
  3.5 27.2 %collective-permute-start.10 = (f32[128,1024]{1,0:T(8,128)S(1)}, f32[128,1024]{1,0:T(8,128)S(1)}, u32[]{:S(2)}, u32[]{:S(2)}) collective-permute-start(f32[128,1024]{1,0:T(8,128)S(1)} %get-tuple-element.36), channel_id=1, source_target_pairs={{1,2},{2,1},{5,6},{6,5},{9,10},{10,9},{13,14},{14,13},{17,18},{18,... | collective-permute-start | bytes 1572872 | tf_op jit(solution)/shard_map/ppermute | solution.py:205
  5.8 27.2 %collective-permute-start.13 = (f32[128,1024]{1,0:T(8,128)S(1)}, f32[128,1024]{1,0:T(8,128)S(1)}, u32[]{:S(2)}, u32[]{:S(2)}) collective-permute-start(f32[128,1024]{1,0:T(8,128)S(1)} %get-tuple-element.35), channel_id=1, source_target_pairs={{1,2},{2,1},{5,6},{6,5},{9,10},{10,9},{13,14},{14,13},{17,18},{18,... | collective-permute-start | bytes 1572872 | tf_op jit(solution)/shard_map/ppermute | solution.py:205
  16.3 18.3 %collective-permute-start.24 = (f32[128,1024]{1,0:T(8,128)S(1)}, f32[128,1024]{1,0:T(8,128)S(1)}, u32[]{:S(2)}, u32[]{:S(2)}) collective-permute-start(f32[128,1024]{1,0:T(8,128)S(1)} %collective-permute-done.refs_0_.refs_4_), channel_id=1, source_target_pairs={{0,8},{5,13},{10,2},{15,7},{16,24},{21,29},{26,18},{31,23}} | collective-permute-start | bytes 1572872 | tf_op jit(solution)/shard_map/ppermute | solution.py:205
  26.4 11.1 %collective-permute-start.25 = (f32[128,1024]{1,0:T(8,128)S(1)}, f32[128,1024]{1,0:T(8,128)S(1)}, u32[]{:S(2)}, u32[]{:S(2)}) collective-permute-start(f32[128,1024]{1,0:T(8,128)S(1)} %collective-permute-done.4.refs_1_.refs_5_), channel_id=1, source_target_pairs={{0,8},{5,13},{10,2},{15,7},{16,24},{21,29},{26,18},{31,23}} | collective-permute-start | bytes 1572872 | tf_op jit(solution)/shard_map/ppermute | solution.py:205
  28.8 13.1 %collective-permute-start.5 = (f32[128,1024]{1,0:T(8,128)S(1)}, f32[128,1024]{1,0:T(8,128)}, u32[]{:S(2)}, u32[]{:S(2)}) collective-permute-start(f32[128,1024]{1,0:T(8,128)S(1)} %collective-permute-done.4.refs_1_.refs_5_), channel_id=1, source_target_pairs={{1,2},{2,1},{5,6},{6,5},{9,10},{10,9},{13,14},{14,13},{17,18},{18,... | collective-permute-start | bytes 1572872 | tf_op jit(solution)/shard_map/ppermute | solution.py:205
  30.7 45.2 %collective-permute-start.30 = (f32[256,1024]{1,0:T(8,128)}, f32[256,1024]{1,0:T(8,128)}, u32[]{:S(2)}, u32[]{:S(2)}) collective-permute-start(f32[256,1024]{1,0:T(8,128)} %refs_2_.1), channel_id=1, source_target_pairs={{0,8},{5,13},{10,2},{15,7},{16,24},{21,29},{26,18},{31,23}} | collective-permute-start | bytes 3145736 | tf_op jit(solution)/shard_map/ppermute | solution.py:205
  33.0 43.5 %collective-permute-start.22 = (f32[256,1024]{1,0:T(8,128)}, f32[256,1024]{1,0:T(8,128)}, u32[]{:S(2)}, u32[]{:S(2)}) collective-permute-start(f32[256,1024]{1,0:T(8,128)} %refs_2_.1), channel_id=1, source_target_pairs={{0,16},{1,17},{2,18},{3,19},{4,20},{5,21},{6,22},{7,23},{8,24},{9,... | collective-permute-start | bytes 3145736 | tf_op jit(solution)/shard_map/ppermute | solution.py:205
  35.3 13.6 %collective-permute-start.11 = (f32[128,1024]{1,0:T(8,128)S(1)}, f32[128,1024]{1,0:T(8,128)S(1)}, u32[]{:S(2)}, u32[]{:S(2)}) collective-permute-start(f32[128,1024]{1,0:T(8,128)S(1)} %collective-permute-done.10.refs_1_), channel_id=1, source_target_pairs={{1,0},{2,3},{5,4},{6,7},{9,8},{10,11},{13,12},{14,15},{17,16},{18,... | collective-permute-start | bytes 1572872 | tf_op jit(solution)/shard_map/ppermute | solution.py:205
  36.7 0.8 copy-start.10
  37.5 0.8 copy-start.8
  38.3 21.0 %collective-permute-start.14 = (f32[128,1024]{1,0:T(8,128)S(1)}, f32[128,1024]{1,0:T(8,128)S(1)}, u32[]{:S(2)}, u32[]{:S(2)}) collective-permute-start(f32[128,1024]{1,0:T(8,128)S(1)} %collective-permute-done.13.refs_2_), channel_id=1, source_target_pairs={{1,0},{2,3},{5,4},{6,7},{9,8},{10,11},{13,12},{14,15},{17,16},{18,... | collective-permute-start | bytes 1572872 | tf_op jit(solution)/shard_map/ppermute | solution.py:205
  41.9 23.4 %collective-permute-start.1 = (f32[128,1024]{1,0:T(8,128)S(1)}, f32[128,1024]{1,0:T(8,128)S(1)}, u32[]{:S(2)}, u32[]{:S(2)}) collective-permute-start(f32[128,1024]{1,0:T(8,128)S(1)} %collective-permute-done.refs_0_.refs_4_), channel_id=1, source_target_pairs={{1,2},{2,1},{5,6},{6,5},{9,10},{10,9},{13,14},{14,13},{17,18},{18,... | collective-permute-start | bytes 1572872 | tf_op jit(solution)/shard_map/ppermute | solution.py:205
  49.7 28.1 %collective-permute-start.28 = (f32[128,1024]{1,0:T(8,128)S(1)}, f32[128,1024]{1,0:T(8,128)}, u32[]{:S(2)}, u32[]{:S(2)}) collective-permute-start(f32[128,1024]{1,0:T(8,128)S(1)} %collective-permute-done.refs_0_.refs_4_), channel_id=1, source_target_pairs={{0,16},{1,17},{2,18},{3,19},{4,20},{5,21},{6,22},{7,23},{8,24},{9,... | collective-permute-start | bytes 1572872 | tf_op jit(solution)/shard_map/ppermute | solution.py:205
  60.1 19.1 %collective-permute-start.6 = (f32[128,1024]{1,0:T(8,128)}, f32[128,1024]{1,0:T(8,128)}, u32[]{:S(2)}, u32[]{:S(2)}) collective-permute-start(f32[128,1024]{1,0:T(8,128)} %collective-permute-done.5.refs_0_), channel_id=1, source_target_pairs={{1,0},{2,3},{5,4},{6,7},{9,8},{10,11},{13,12},{14,15},{17,16},{18,... | collective-permute-start | bytes 1572872 | tf_op jit(solution)/shard_map/ppermute | solution.py:205
  65.3 21.3 %collective-permute-start.2 = (f32[128,1024]{1,0:T(8,128)S(1)}, f32[128,1024]{1,0:T(8,128)}, u32[]{:S(2)}, u32[]{:S(2)}) collective-permute-start(f32[128,1024]{1,0:T(8,128)S(1)} %collective-permute-done.1.refs_0_), channel_id=1, source_target_pairs={{1,0},{2,3},{5,4},{6,7},{9,8},{10,11},{13,12},{14,15},{17,16},{18,... | collective-permute-start | bytes 1572872 | tf_op jit(solution)/shard_map/ppermute | solution.py:205
  67.5 1.0 copy-start.7
  68.5 1.0 copy-start.9
  69.6 38.0 %slice-start = ((s8[8388608]{0:T(1024)(128)(4,1)}), s8[4194304]{0:T(1024)(128)(4,1)S(1)}, s32[]{:S(2)}) async-start(s8[8388608]{0:T(1024)(128)(4,1)} %bitcast.7), calls=%async_computation | async-start | bytes 8388608
  70.2 1.4 copy-start.2
  71.5 1.0 copy-start.5
  72.6 1.0 copy-start.11
  73.6 1.0 copy-start.13
  74.7 24.0 %copy-start.3 = (f32[128,1024]{1,0:T(8,128)S(1)}, f32[128,1024]{1,0:T(8,128)}, u32[]{:S(2)}) copy-start(f32[128,1024]{1,0:T(8,128)} %copy-done.1) | copy-start | bytes 1572868
  75.9 16.1 %collective-permute-start.29 = (f32[128,1024]{1,0:T(8,128)S(1)}, f32[128,1024]{1,0:T(8,128)S(1)}, u32[]{:S(2)}, u32[]{:S(2)}) collective-permute-start(f32[128,1024]{1,0:T(8,128)S(1)} %collective-permute-done.4.refs_1_.refs_5_), channel_id=1, source_target_pairs={{0,16},{1,17},{2,18},{3,19},{4,20},{5,21},{6,22},{7,23},{8,24},{9,... | collective-permute-start | bytes 1572872 | tf_op jit(solution)/shard_map/ppermute | solution.py:205
  76.5 16.2 %collective-permute-start.26 = (f32[128,1024]{1,0:T(8,128)S(1)}, f32[128,1024]{1,0:T(8,128)S(1)}, u32[]{:S(2)}, u32[]{:S(2)}) collective-permute-start(f32[128,1024]{1,0:T(8,128)S(1)} %get-tuple-element.25.refs_0_), channel_id=1, source_target_pairs={{0,4},{2,6},{5,1},{7,3},{8,12},{10,14},{13,9},{15,11},{16,20},{18,... | collective-permute-start | bytes 1572872 | tf_op jit(solution)/shard_map/ppermute | solution.py:205
  77.9 16.1 %collective-permute-start.27 = (f32[128,1024]{1,0:T(8,128)S(1)}, f32[128,1024]{1,0:T(8,128)S(1)}, u32[]{:S(2)}, u32[]{:S(2)}) collective-permute-start(f32[128,1024]{1,0:T(8,128)S(1)} %get-tuple-element.26.refs_1_), channel_id=1, source_target_pairs={{0,4},{2,6},{5,1},{7,3},{8,12},{10,14},{13,9},{15,11},{16,20},{18,... | collective-permute-start | bytes 1572872 | tf_op jit(solution)/shard_map/ppermute | solution.py:205
  79.2 16.2 %collective-permute-start.18 = (f32[128,1024]{1,0:T(8,128)S(1)}, f32[128,1024]{1,0:T(8,128)S(1)}, u32[]{:S(2)}, u32[]{:S(2)}) collective-permute-start(f32[128,1024]{1,0:T(8,128)S(1)} %get-tuple-element.21.refs_0_.refs_4_), channel_id=1, source_target_pairs={{0,8},{5,13},{10,2},{15,7},{16,24},{21,29},{26,18},{31,23}} | collective-permute-start | bytes 1572872 | tf_op jit(solution)/shard_map/ppermute | solution.py:205
  86.6 21.0 %slice-start.1 = ((s8[8388608]{0:T(1024)(128)(4,1)}), s8[4194304]{0:T(1024)(128)(4,1)S(1)}, s32[]{:S(2)}) async-start(s8[8388608]{0:T(1024)(128)(4,1)} %bitcast.7), calls=%async_computation.1 | async-start | bytes 8388608
  86.6 10.1 %collective-permute-start.19 = (f32[128,1024]{1,0:T(8,128)S(1)}, f32[128,1024]{1,0:T(8,128)S(1)}, u32[]{:S(2)}, u32[]{:S(2)}) collective-permute-start(f32[128,1024]{1,0:T(8,128)S(1)} %get-tuple-element.22.refs_1_.refs_5_), channel_id=1, source_target_pairs={{0,8},{5,13},{10,2},{15,7},{16,24},{21,29},{26,18},{31,23}} | collective-permute-start | bytes 1572872 | tf_op jit(solution)/shard_map/ppermute | solution.py:205
  92.1 12.2 %collective-permute-start.15 = (f32[128,1024]{1,0:T(8,128)S(1)}, f32[128,1024]{1,0:T(8,128)S(1)}, u32[]{:S(2)}, u32[]{:S(2)}) collective-permute-start(f32[128,1024]{1,0:T(8,128)S(1)} %get-tuple-element.20), channel_id=1, source_target_pairs={{0,16},{1,17},{2,18},{3,19},{4,20},{5,21},{6,22},{7,23},{8,24},{9,... | collective-permute-start | bytes 1572872 | tf_op jit(solution)/shard_map/ppermute | solution.py:205
  92.7 12.1 %collective-permute-start.7 = (f32[128,1024]{1,0:T(8,128)S(1)}, f32[128,1024]{1,0:T(8,128)S(1)}, u32[]{:S(2)}, u32[]{:S(2)}) collective-permute-start(f32[128,1024]{1,0:T(8,128)S(1)} %shard_map.30.refs_0_.refs_5_), channel_id=1, source_target_pairs={{0,8},{5,13},{10,2},{15,7},{16,24},{21,29},{26,18},{31,23}} | collective-permute-start | bytes 1572872 | tf_op jit(solution)/shard_map/ppermute | solution.py:205
  94.0 21.9 %collective-permute-start.31 = (f32[256,1024]{1,0:T(8,128)S(1)}, f32[256,1024]{1,0:T(8,128)S(1)}, u32[]{:S(2)}, u32[]{:S(2)}) collective-permute-start(f32[256,1024]{1,0:T(8,128)S(1)} %shard_map.36.refs_0_), channel_id=1, source_target_pairs={{0,4},{2,6},{5,1},{7,3},{8,12},{10,14},{13,9},{15,11},{16,20},{18,... | collective-permute-start | bytes 3145736 | tf_op jit(solution)/shard_map/ppermute | solution.py:205
  95.4 10.9 %collective-permute-start.3 = (f32[128,1024]{1,0:T(8,128)S(1)}, f32[128,1024]{1,0:T(8,128)S(1)}, u32[]{:S(2)}, u32[]{:S(2)}) collective-permute-start(f32[128,1024]{1,0:T(8,128)S(1)} %shard_map.28.refs_0_.refs_4_), channel_id=1, source_target_pairs={{0,8},{5,13},{10,2},{15,7},{16,24},{21,29},{26,18},{31,23}} | collective-permute-start | bytes 1572872 | tf_op jit(solution)/shard_map/ppermute | solution.py:205
  96.7 41.9 %collective-permute-start.23 = (f32[256,1024]{1,0:T(8,128)}, f32[256,1024]{1,0:T(8,128)S(1)}, u32[]{:S(2)}, u32[]{:S(2)}) collective-permute-start(f32[256,1024]{1,0:T(8,128)} %collective-permute-done.22.refs_3_), channel_id=1, source_target_pairs={{1,2},{2,1},{5,6},{6,5},{9,10},{10,9},{13,14},{14,13},{17,18},{18,... | collective-permute-start | bytes 3145736 | tf_op jit(solution)/shard_map/ppermute | solution.py:205
  99.9 10.4 %copy-start.14 = (f32[128,1024]{1,0:T(8,128)}, f32[128,1024]{1,0:T(8,128)S(1)}, u32[]{:S(2)}) copy-start(f32[128,1024]{1,0:T(8,128)S(1)} %get-tuple-element.24.refs_1_) | copy-start | bytes 1572868
  104.2 11.0 %collective-permute-start.12 = (f32[128,1024]{1,0:T(8,128)S(1)}, f32[128,1024]{1,0:T(8,128)S(1)}, u32[]{:S(2)}, u32[]{:S(2)}) collective-permute-start(f32[128,1024]{1,0:T(8,128)S(1)} %shard_map.32), channel_id=1, source_target_pairs={{0,16},{1,17},{2,18},{3,19},{4,20},{5,21},{6,22},{7,23},{8,24},{9,... | collective-permute-start | bytes 1572872 | tf_op jit(solution)/shard_map/ppermute | solution.py:205
  104.8 19.1 %collective-permute-start.20 = (f32[128,1024]{1,0:T(8,128)S(1)}, f32[128,1024]{1,0:T(8,128)S(1)}, u32[]{:S(2)}, u32[]{:S(2)}) collective-permute-start(f32[128,1024]{1,0:T(8,128)S(1)} %get-tuple-element.23.refs_0_), channel_id=1, source_target_pairs={{0,4},{2,6},{5,1},{7,3},{8,12},{10,14},{13,9},{15,11},{16,20},{18,... | collective-permute-start | bytes 1572872 | tf_op jit(solution)/shard_map/ppermute | solution.py:205
  106.3 19.8 %collective-permute-start.21 = (f32[128,1024]{1,0:T(8,128)S(1)}, f32[128,1024]{1,0:T(8,128)S(1)}, u32[]{:S(2)}, u32[]{:S(2)}) collective-permute-start(f32[128,1024]{1,0:T(8,128)S(1)} %get-tuple-element.24.refs_1_), channel_id=1, source_target_pairs={{0,4},{2,6},{5,1},{7,3},{8,12},{10,14},{13,9},{15,11},{16,20},{18,... | collective-permute-start | bytes 1572872 | tf_op jit(solution)/shard_map/ppermute | solution.py:205
  115.2 32.8 %collective-permute-start.17 = (f32[128,1024]{1,0:T(8,128)}, f32[128,1024]{1,0:T(8,128)S(1)}, u32[]{:S(2)}, u32[]{:S(2)}) collective-permute-start(f32[128,1024]{1,0:T(8,128)} %collective-permute-done.6.refs_1_), channel_id=1, source_target_pairs={{0,16},{3,19},{4,20},{7,23},{8,24},{11,27},{12,28},{15,31},{16,0},... | collective-permute-start | bytes 1572872 | tf_op jit(solution)/shard_map/ppermute | solution.py:205
  115.9 32.1 %collective-permute-start.16 = (f32[128,1024]{1,0:T(8,128)S(1)}, f32[128,1024]{1,0:T(8,128)}, u32[]{:S(2)}, u32[]{:S(2)}) collective-permute-start(f32[128,1024]{1,0:T(8,128)S(1)} %collective-permute-done.12.refs_7_.refs_4_), channel_id=1, source_target_pairs={{1,0},{2,3},{5,4},{6,7},{9,8},{10,11},{13,12},{14,15},{17,16},{18,... | collective-permute-start | bytes 1572872 | tf_op jit(solution)/shard_map/ppermute | solution.py:205
  124.7 18.4 %collective-permute-start.9 = (f32[128,1024]{1,0:T(8,128)S(1)}, f32[128,1024]{1,0:T(8,128)S(1)}, u32[]{:S(2)}, u32[]{:S(2)}) collective-permute-start(f32[128,1024]{1,0:T(8,128)S(1)} %shard_map.31.refs_1_), channel_id=1, source_target_pairs={{0,4},{2,6},{5,1},{7,3},{8,12},{10,14},{13,9},{15,11},{16,20},{18,... | collective-permute-start | bytes 1572872 | tf_op jit(solution)/shard_map/ppermute | solution.py:205
  126.8 16.3 %collective-permute-start.8 = (f32[128,1024]{1,0:T(8,128)S(1)}, f32[128,1024]{1,0:T(8,128)S(1)}, u32[]{:S(2)}, u32[]{:S(2)}) collective-permute-start(f32[128,1024]{1,0:T(8,128)S(1)} %shard_map.29.refs_0_), channel_id=1, source_target_pairs={{0,4},{2,6},{5,1},{7,3},{8,12},{10,14},{13,9},{15,11},{16,20},{18,... | collective-permute-start | bytes 1572872 | tf_op jit(solution)/shard_map/ppermute | solution.py:205
  133.5 5.1 %copy-start.15 = (f32[128,1024]{1,0:T(8,128)S(1)}, f32[128,1024]{1,0:T(8,128)}, u32[]{:S(2)}) copy-start(f32[128,1024]{1,0:T(8,128)} %copy-done.14) | copy-start | bytes 1572868
  133.5 5.1 %copy-start.17 = (f32[128,1024]{1,0:T(8,128)S(1)}, f32[128,1024]{1,0:T(8,128)}, u32[]{:S(2)}) copy-start(f32[128,1024]{1,0:T(8,128)} %copy-done.16) | copy-start | bytes 1572868
  133.5 5.1 %copy-start.19 = (f32[128,1024]{1,0:T(8,128)S(1)}, f32[128,1024]{1,0:T(8,128)}, u32[]{:S(2)}) copy-start(f32[128,1024]{1,0:T(8,128)} %copy-done.18) | copy-start | bytes 1572868
  (6 other events, 4.8 us)

commit v2 on v0

v2 whole, which is shorter than its diff:
```python
import jax
import jax.numpy as jnp
from jax import lax
from jax.experimental import pallas as pl
from jax.experimental.pallas import tpu as pltpu
from jax.sharding import PartitionSpec as P

AXES = ("row", "col", "layer")
F32, BF16 = jnp.float32, jnp.bfloat16
VMEM = pl.BlockSpec(memory_space=pltpu.VMEM)
SMEM = pl.BlockSpec(memory_space=pltpu.SMEM)
HBM = pl.BlockSpec(memory_space=pltpu.HBM)
ANY = pl.BlockSpec(memory_space=pl.ANY)
SUM_MIB, FINISH_MIB = 16, 24


def split(x):
    high = x.astype(BF16)
    return high, (x - high.astype(F32)).astype(BF16)


def left_stack(x):
    high, low = split(x)
    return jnp.concatenate([high, high, low], 0)


def right_stack(x):
    high, low = split(x)
    return jnp.concatenate([high, low, high], 0)


def dot(left, right):
    return lax.dot_general(left, right, (((0,), (0,)), ((), ())), preferred_element_type=F32)


def params(mib):
    return pltpu.CompilerParams(vmem_limit_bytes=mib << 20, has_side_effects=True)


def cost(flops):
    return pl.CostEstimate(flops=flops, bytes_accessed=1 << 20, transcendentals=0)


def call(kernel, args, outs, aliases=None, scratch=(), flops=1 << 20, mib=40):
    return pl.pallas_call(
        kernel,
        in_specs=[spec for _, spec in args],
        out_specs=[spec for _, spec in outs],
        out_shape=[shape for shape, _ in outs],
        input_output_aliases=aliases or {},
        scratch_shapes=scratch,
        compiler_params=params(mib),
        cost_estimate=cost(flops),
    )(*(a for a, _ in args))


def load(flags, c, own, other, sems):
    width = own.shape[1]
    row = flags[0]
    halves = [(row, own, 0), (1 - row, other, 1)]
    copies = [
        pltpu.make_async_copy(c.at[:, pl.ds(pl.multiple_of(i * width, width), width)], to, sems.at[k])
        for i, to, k in halves
    ]
    for copy in copies:
        copy.start()
    for copy in copies:
        copy.wait()


def mark(flags, out):
    out[...] = jnp.full(out.shape, flags[0])


def part(x, first, second):
    at = first.shape[0]
    first[...] = x[:at]
    second[...] = x[at:]


def select(which, flags, firsts, seconds):
    windows = [s if isinstance(s, tuple) else (s, 0) for s in seconds]
    n = len(firsts)

    def kernel(flag_ref, *refs):
        outs = refs[2 * n :]

        @pl.when(flag_ref[which] == 1)
        def _():
            for source, out in zip(refs[:n], outs, strict=True):
                out[...] = source[...]

        @pl.when(flag_ref[which] != 1)
        def _():
            for source, (_, start), out in zip(refs[n : 2 * n], windows, outs, strict=True):
                out[...] = source[start : start + out.shape[0]]

    outs = [(pltpu.VMEM(a.shape, F32), VMEM) for a in firsts]
    args = [(flags, SMEM)] + [(a, VMEM) for a in (*firsts, *(a for a, _ in windows))]
    return call(kernel, args, outs, mib=8)


class Operand:
    def __init__(self, *groups):
        listed = lambda c: c if isinstance(c, tuple) else (c,)
        self.groups = [(g[0], [listed(c) for c in g[1]]) if isinstance(g, tuple) else (None, [(g,)]) for g in groups]
        self.rows = sum(a.shape[0] for _, choices in self.groups for a in choices[0])
        self.arrays = [a for _, choices in self.groups for c in choices for a in c]
        self.plain = len(self.arrays) == 1

    def scratch(self, width):
        return [] if self.plain else [pltpu.VMEM((self.rows, width), F32)]

    def settle(self, flags, refs, scratch):
        if self.plain:
            return refs.pop(0)
        to, start = scratch.pop(0), 0
        for which, choices in self.groups:
            for i, arrays in enumerate(choices):
                sources = [refs.pop(0) for _ in arrays]

                def copy(sources=sources, row=start):
                    for source in sources:
                        to[row : row + source.shape[0]] = source[...]
                        row += source.shape[0]

                copy() if which is None else pl.when(flags[which] == i)(copy)
            start += sum(a.shape[0] for a in choices[0])
        return to


def accumulate(flags, left, rights, accs, tile=256):
    n = len(accs)
    operands = [left, *rights]
    arrays = [a for p in operands for a in p.arrays]
    width = accs[0].shape[1]

    def kernel(flag_ref, *refs):
        refs, olds, rest = list(refs[: len(arrays)]), refs[len(arrays) :][:n], refs[len(arrays) + n :]
        news, scratch = rest[:n], list(rest[n:])
        held = [p.settle(flag_ref, refs, scratch) for p in operands]
        stack = left_stack(held[0][...])
        for i in range(n):
            for j in range(0, width, tile):
                cols = slice(j, j + tile)
                news[i][:, cols] = olds[i][:, cols] + dot(stack, right_stack(held[1 + i][:, cols]))

    args = [(flags, SMEM)] + [(a, VMEM) for a in arrays] + [(a, VMEM) for a in accs]
    outs = [(pltpu.VMEM(a.shape, F32), VMEM) for a in accs]
    first = 1 + len(arrays)
    scratch = [s for p in operands for s in p.scratch(width)]
    flops = sum(6 * left.rows * a.shape[0] * a.shape[1] for a in accs)
    return call(kernel, args, outs, {first + i: i for i in range(n)}, scratch, flops=flops, mib=SUM_MIB)


def finish(flags, left, rights, accs, halves, shape, tile=128):
    operands = [left, *rights]
    arrays = [a for p in operands for a in p.arrays]
    height, width = accs[0].shape
    tiles, n = height // tile, len(accs)

    def kernel(flag_ref, *refs):
        olds, rest = refs[len(arrays) :][:n], list(refs[len(arrays) + n :])
        out, ready, sems = rest[0], rest[-2], rest[-1]
        refs, scratch = list(refs[: len(arrays)]), rest[1:-2]
        held = [p.settle(flag_ref, refs, scratch) for p in operands]
        stack = left_stack(held[0][...])
        copies = []
        for k in range(n):
            right = right_stack(held[1 + k][...])
            cols = pl.ds(pl.multiple_of(flag_ref[halves[k]] * width, width), width)
            for i in range(tiles):
                rows = slice(i * tile, (i + 1) * tile)
                ready[k, rows] = olds[k][rows] + dot(stack[:, rows], right)
                copies.append(pltpu.make_async_copy(ready.at[k, rows], out.at[rows, cols], sems.at[k, i]))
                copies[-1].start()
        for copy in copies:
            copy.wait()

    args = [(flags, SMEM)] + [(a, VMEM) for a in arrays] + [(a, VMEM) for a in accs]
    scratch = [s for p in operands for s in p.scratch(width)]
    scratch += [pltpu.VMEM((n, height, width), F32), pltpu.SemaphoreType.DMA((n, tiles))]
    flops = 6 * left.rows * height * width * n
    (out,) = call(kernel, args, [(jax.ShapeDtypeStruct(shape, F32), ANY)], scratch=scratch, flops=flops, mib=FINISH_MIB)
    return out


def paired(mesh, panel, c_in):
    n_row, n_col, n_layer = (mesh.shape[a] for a in AXES)

    def send(x, to):
        pairs = []
        for r in range(n_row):
            for c in range(n_col):
                for l in range(n_layer):
                    target = to(r, c, l)
                    if target is not None:
                        a, b, d = target
                        pairs.append(((r * n_col + c) * n_layer + l, (a * n_col + b) * n_layer + d))
        return lax.ppermute(x, AXES, pairs)

    inner = lambda l: l in (1, 2)
    near = lambda r, c, l: (r, c, l ^ 1)
    outward = lambda r, c, l: (r, c, l ^ 1) if inner(l) else None
    middle = lambda r, c, l: (r, c, 3 - l) if inner(l) else None
    swap = lambda r, c, l: (1 - r, c, l)
    swap_ends = lambda r, c, l: None if inner(l) else (1 - r, c, l)
    across = lambda r, c, l: (r, c ^ 2, l) if c == l else None
    beside = lambda r, c, l: (r, c ^ 1, l) if c == l else None
    beyond = lambda r, c, l: (r, c ^ 1, l) if c == l ^ 2 else None

    row, col, layer = (lax.axis_index(a) for a in AXES)
    place = col ^ layer
    flags = jnp.stack([row, 1 - row, (layer == 1) | (layer == 2), place == 0, place & 1, place]).astype(jnp.int32)
    ROW, OTHER_ROW, INNER, _, _, PLACE = range(6)

    depth, width = panel.shape
    cut = depth * CUT // 16
    c_flat = c_in.reshape(c_in.shape[2:])

    b1 = send(panel, middle)
    a1 = send(panel, near)
    x1 = send(panel, swap)
    y0 = send(panel, across)
    acc = [(pltpu.VMEM((c_flat.shape[0], width), F32), VMEM)] * 2
    own, other = call(load, [(flags, SMEM), (c_flat, HBM)], acc, scratch=[pltpu.SemaphoreType.DMA((2,))], mib=20)
    e0 = send(panel, beside)
    f0 = send(y0, beyond)

    a2 = send(b1, outward)
    call(mark, [(flags, SMEM)], [(pltpu.VMEM((8, 128), jnp.int32), VMEM)], mib=1)
    parts = [(pltpu.VMEM((n, width), F32), VMEM) for n in (cut, depth - cut)]
    p1a, p1b = call(part, [(a1, VMEM)], parts, mib=8)
    b2a = send(p1a, middle)
    x2 = send(a1, swap)
    b2b = send(p1b, middle)
    y1 = send(a1, across)
    e1 = send(a1, beside)
    b3 = send(x1, middle)
    left = Operand((PLACE, (panel, e0, y0, f0)))
    own, other = accumulate(flags, left, [Operand(panel), Operand(x1)], [own, other])

    a3a = send(b2a, outward)
    f1 = send(y1, beyond)
    (s3a,) = select(INNER, flags, [b2a], [a2])
    x3a = send(s3a, swap)
    a3b = send(b2b, outward)
    s3b, p2 = select(INNER, flags, [b2b, b1], [(a2, cut), a2])
    x3b = send(s3b, swap)
    y2 = send(p2, across)
    e2 = send(p2, beside)
    left = Operand((PLACE, (a1, e1, y1, f1)))
    own, other = accumulate(flags, left, [Operand(a1), Operand(x2)], [own, other])

    (p3a,) = select(INNER, flags, [b2a], [a3a])
    y3a = send(p3a, across)
    e3a = send(p3a, beside)
    a4 = send(x3a, outward)
    f2 = send(y2, beyond)
    (p3b,) = select(INNER, flags, [b2b], [a3b])
    y3b = send(p3b, across)
    x4 = send(a3b, swap_ends)
    e3b = send(p3b, beside)
    f3a = send(y3a, beyond)
    f3b = send(y3b, beyond)
    left = Operand((PLACE, (p2, e2, y2, f2)))
    q2 = Operand((INNER, ((x3a, x3b), (b3,))))
    own, other = accumulate(flags, left, [Operand(p2), q2], [own, other])
    left = Operand((PLACE, ((p3a, p3b), (e3a, e3b), (y3a, y3b), (f3a, f3b))))
    q3 = Operand((INNER, (a4, x3a)), (INNER, (x4, x3b)))
    halves = [ROW, OTHER_ROW]
    out = finish(flags, left, [Operand(p3a, p3b), q3], [own, other], halves, c_flat.shape)
    return out.reshape(c_in.shape)


CUT = 10


def gathered(panel, c_in):
    rows_here, width = c_in.shape[0], panel.shape[1]
    own = lax.all_gather(panel, "layer", axis=0, tiled=True)
    right = lax.all_gather(own, "row", axis=1, tiled=True)
    columns = lax.all_gather(own, "col", axis=0)
    mine = lax.dynamic_slice_in_dim(columns, lax.axis_index("layer") * rows_here, rows_here, 0)
    left = jnp.moveaxis(mine, 0, 1).reshape(own.shape[0], rows_here * width)
    tile = lax.dot_general(
        left, right, (((0,), (0,)), ((), ())), precision=lax.Precision.HIGHEST, preferred_element_type=F32
    )
    return c_in + tile.reshape(c_in.shape)


def solution(mesh):
    placed = (P("layer", ("col", "row")), P("layer", "row", None, "col"))
    fits = tuple(mesh.shape[a] for a in AXES) == (2, 4, 4)

    def on_device(panel, c_in):
        if not fits:
            return gathered(panel, c_in)
        return paired(mesh, panel, c_in)

    return jax.shard_map(
        on_device,
        mesh=mesh,
        in_specs=placed,
        out_specs=P("layer", "row", None, "col"),
        check_vma=False,
    )
```

time: 684 us -> 146 us (0.21)
  the two profiles are of different devices: /device:TPU:0 before, /device:TPU:29 now
where the time goes in v2:
time: 146 us; the launch traced here: 145 us
  waiting for transfers between devices  65.8 us (45%)
  starting transfers between devices  47.4 us (32%)
  Pallas kernels  28.8 us (20%)
  local copies, waits for them, and re-layouts  2.4 us (2%)
    ppermute x29, waiting for transfers between devices, send(): return lax.ppermute(x, AXES, pairs)  65.8 us
    ppermute x29, starting transfers between devices, send(): return lax.ppermute(x, AXES, pairs)  47.4 us
    pallas_call x11, Pallas kernels, call(): pl.pallas_call(kernel, in_specs=[spec for _, spec in args], out_specs=[sp...  28.8 us
  transfers between devices with their start and end apart: 29, of which 6 were waited for; matrix products, arithmetic and copies ran while one was open for 0% of the time, Pallas kernels for 16%

profile of v2, /device:TPU:29, one launch (start us, length us, event | category | flops | bytes accessed | tf_op | source)
XLA Modules:
  0.0 145.0 jit_solution(14520359503202900771)
XLA Ops:
  0.0 0.7 collective-permute-start.11
  0.7 1.6 %collective-permute-start = (f32[256,1024]{1,0:T(8,128)}, f32[256,1024]{1,0:T(8,128)S(1)}, u32[]{:S(2)}, u32[]{:S(2)}) collective-permute-start(f32[256,1024]{1,0:T(8,128)} %refs_4_.1), channel_id=1, source_target_pairs={{0,1},{1,0},{2,3},{3,2},{4,5},{5,4},{6,7},{7,6},{8,9},{9,8},{10,11... | collective-permute-start | bytes 3145736 | tf_op jit(solution)/shard_map/ppermute | solution.py:200
  2.3 3.1 %collective-permute-start.27 = (f32[256,1024]{1,0:T(8,128)}, f32[256,1024]{1,0:T(8,128)}, u32[]{:S(2)}, u32[]{:S(2)}) collective-permute-start(f32[256,1024]{1,0:T(8,128)} %refs_4_.1), channel_id=1, source_target_pairs={{0,8},{5,13},{10,2},{15,7},{16,24},{21,29},{26,18},{31,23}} | collective-permute-start | bytes 3145736 | tf_op jit(solution)/shard_map/ppermute | solution.py:200
  5.4 1.2 collective-permute-start.20
  6.6 2.0 %collective-permute-start.26 = (f32[256,1024]{1,0:T(8,128)}, f32[256,1024]{1,0:T(8,128)S(1)}, u32[]{:S(2)}, u32[]{:S(2)}) collective-permute-start(f32[256,1024]{1,0:T(8,128)} %refs_4_.1), channel_id=1, source_target_pairs={{0,4},{5,1},{10,14},{15,11},{16,20},{21,17},{26,30},{31,27}} | collective-permute-start | bytes 3145736 | tf_op jit(solution)/shard_map/ppermute | solution.py:200
  8.7 1.3 collective-permute-start.12
  10.0 15.3 %collective-permute-done.x.refs_0_.refs_4_ = f32[256,1024]{1,0:T(8,128)S(1)} collective-permute-done((f32[256,1024]{1,0:T(8,128)}, f32[256,1024]{1,0:T(8,128)S(1)}, u32[]{:S(2)}, u32[]{:S(2)}) %collective-permute-start) | collective-permute-done | bytes 1048608 | tf_op jit(solution)/shard_map/ppermute | solution.py:200
  25.3 0.7 collective-permute-start.1
  26.0 0.7 collective-permute-start.3
  26.7 4.0 %collective-permute-done.20.refs_5_ = f32[256,1024]{1,0:T(8,128)} collective-permute-done((f32[256,1024]{1,0:T(8,128)}, f32[256,1024]{1,0:T(8,128)}, u32[]{:S(2)}, u32[]{:S(2)}) %collective-permute-start.20) | collective-permute-done | bytes 1048608 | tf_op jit(solution)/shard_map/ppermute | solution.py:200
  30.7 1.6 %collective-permute-start.28 = (f32[256,1024]{1,0:T(8,128)}, f32[256,1024]{1,0:T(8,128)}, u32[]{:S(2)}, u32[]{:S(2)}) collective-permute-start(f32[256,1024]{1,0:T(8,128)} %collective-permute-done.27.refs_2_), channel_id=1, source_target_pairs={{2,6},{7,3},{8,12},{13,9},{18,22},{23,19},{24,28},{29,25}} | collective-permute-start | bytes 3145736 | tf_op jit(solution)/shard_map/ppermute | solution.py:200
  32.3 1.3 collective-permute-start.4
  33.6 1.1 copy-done.2
  34.7 3.2 %collective-permute-start.23 = (f32[256,1024]{1,0:T(8,128)S(1)}, f32[256,1024]{1,0:T(8,128)}, u32[]{:S(2)}, u32[]{:S(2)}) collective-permute-start(f32[256,1024]{1,0:T(8,128)S(1)} %collective-permute-done.x.refs_0_.refs_4_), channel_id=1, source_target_pairs={{0,8},{5,13},{10,2},{15,7},{16,24},{21,29},{26,18},{31,23}} | collective-permute-start | bytes 3145736 | tf_op jit(solution)/shard_map/ppermute | solution.py:200
  37.9 2.3 %collective-permute-start.22 = (f32[256,1024]{1,0:T(8,128)S(1)}, f32[256,1024]{1,0:T(8,128)}, u32[]{:S(2)}, u32[]{:S(2)}) collective-permute-start(f32[256,1024]{1,0:T(8,128)S(1)} %collective-permute-done.x.refs_0_.refs_4_), channel_id=1, source_target_pairs={{0,4},{5,1},{10,14},{15,11},{16,20},{21,17},{26,30},{31,27}} | collective-permute-start | bytes 3145736 | tf_op jit(solution)/shard_map/ppermute | solution.py:200
  40.2 21.3 %collective-permute-done.4.refs_1_ = f32[96,1024]{1,0:T(8,128)S(1)} collective-permute-done((f32[96,1024]{1,0:T(8,128)S(1)}, f32[96,1024]{1,0:T(8,128)S(1)}, u32[]{:S(2)}, u32[]{:S(2)}) %collective-permute-start.4) | collective-permute-done | bytes 393248 | tf_op jit(solution)/shard_map/ppermute | solution.py:200
  61.5 1.2 collective-permute-start.25
  62.7 1.7 %collective-permute-start.21 = (f32[256,1024]{1,0:T(8,128)}, f32[256,1024]{1,0:T(8,128)}, u32[]{:S(2)}, u32[]{:S(2)}) collective-permute-start(f32[256,1024]{1,0:T(8,128)} %collective-permute-done.20.refs_5_), channel_id=1, source_target_pairs={{1,2},{2,1},{5,6},{6,5},{9,10},{10,9},{13,14},{14,13},{17,18},{18,... | collective-permute-start | bytes 3145736 | tf_op jit(solution)/shard_map/ppermute | solution.py:200
  64.4 0.1 stack.35.flags.flag_ref
  64.5 1.2 copy-done.5
  65.7 0.6 shard_map.33
  66.4 2.5 %collective-permute-start.18 = (f32[256,1024]{1,0:T(8,128)S(1)}, f32[256,1024]{1,0:T(8,128)S(1)}, u32[]{:S(2)}, u32[]{:S(2)}) collective-permute-start(f32[256,1024]{1,0:T(8,128)S(1)} %get-tuple-element.20.refs_0_.refs_4_), channel_id=1, source_target_pairs={{0,8},{5,13},{10,2},{15,7},{16,24},{21,29},{26,18},{31,23}} | collective-permute-start | bytes 3145736 | tf_op jit(solution)/shard_map/ppermute | solution.py:200
  68.8 0.6 shard_map.31.refs_1_.refs_9_
  69.4 1.3 collective-permute-start.8
  70.8 1.3 collective-permute-start.2
  72.1 11.4 %collective-permute-done.25.refs_5_ = f32[256,1024]{1,0:T(8,128)} collective-permute-done((f32[256,1024]{1,0:T(8,128)S(1)}, f32[256,1024]{1,0:T(8,128)}, u32[]{:S(2)}, u32[]{:S(2)}) %collective-permute-start.25) | collective-permute-done | bytes 1048608 | tf_op jit(solution)/shard_map/ppermute | solution.py:200
  83.5 5.6 %collective-permute-start.6 = (f32[96,1024]{1,0:T(8,128)S(1)}, f32[96,1024]{1,0:T(8,128)S(1)}, u32[]{:S(2)}, u32[]{:S(2)}) collective-permute-start(f32[96,1024]{1,0:T(8,128)S(1)} %shard_map.31.refs_1_.refs_9_), channel_id=1, source_target_pairs={{0,4},{5,1},{10,14},{15,11},{16,20},{21,17},{26,30},{31,27}} | collective-permute-start | bytes 1179656 | tf_op jit(solution)/shard_map/ppermute | solution.py:200
  89.1 1.3 collective-permute-start.16
  90.4 0.7 collective-permute-start.24
  91.1 1.6 %collective-permute-start.17 = (f32[256,1024]{1,0:T(8,128)S(1)}, f32[256,1024]{1,0:T(8,128)S(1)}, u32[]{:S(2)}, u32[]{:S(2)}) collective-permute-start(f32[256,1024]{1,0:T(8,128)S(1)} %get-tuple-element.20.refs_0_.refs_4_), channel_id=1, source_target_pairs={{0,4},{5,1},{10,14},{15,11},{16,20},{21,17},{26,30},{31,27}} | collective-permute-start | bytes 3145736 | tf_op jit(solution)/shard_map/ppermute | solution.py:200
  92.8 0.7 collective-permute-start.19
  93.5 0.6 shard_map.32
  94.1 0.6 shard_map.30.refs_0_.refs_8_
  94.7 0.3 collective-permute-start.13
  95.1 5.3 %collective-permute-done.16.refs_6_.refs_13_ = f32[96,1024]{1,0:T(8,128)S(1)} collective-permute-done((f32[96,1024]{1,0:T(8,128)S(1)}, f32[96,1024]{1,0:T(8,128)S(1)}, u32[]{:S(2)}, u32[]{:S(2)}) %collective-permute-start.16) | collective-permute-done | bytes 393248 | tf_op jit(solution)/shard_map/ppermute | solution.py:200
  100.3 1.3 collective-permute-start.7
  101.7 1.1 shard_map.28
  102.8 2.6 %shard_map.34 = (f32[1024,1024]{1,0:T(8,128)S(1)}, f32[1024,1024]{1,0:T(8,128)S(1)}) custom-call(s32[6]{0:T(128)S(1)} %stack.35.flags.flag_ref, f32[1024,2048]{1,0:T(8,128)S(1)} %bitcast.8), custom_call_target="tpu_custom_call" | custom-call | flops 1048576 | bytes 1048576 | tf_op jit(solution)/shard_map/pallas_call | solution.py:45
  105.4 8.6 %collective-permute-done.13.refs_5_.refs_11_ = f32[160,1024]{1,0:T(8,128)S(1)} collective-permute-done((f32[160,1024]{1,0:T(8,128)S(1)}, f32[160,1024]{1,0:T(8,128)S(1)}, u32[]{:S(2)}, u32[]{:S(2)}) %collective-permute-start.13) | collective-permute-done | bytes 655392 | tf_op jit(solution)/shard_map/ppermute | solution.py:200
  114.0 2.3 %collective-permute-start.5 = (f32[160,1024]{1,0:T(8,128)S(1)}, f32[160,1024]{1,0:T(8,128)S(1)}, u32[]{:S(2)}, u32[]{:S(2)}) collective-permute-start(f32[160,1024]{1,0:T(8,128)S(1)} %shard_map.30.refs_0_.refs_8_), channel_id=1, source_target_pairs={{0,4},{5,1},{10,14},{15,11},{16,20},{21,17},{26,30},{31,27}} | collective-permute-start | bytes 1966088 | tf_op jit(solution)/shard_map/ppermute | solution.py:200
  116.4 1.3 collective-permute-start.14
  117.7 0.7 collective-permute-start.9
  118.4 5.8 %shard_map.35 = (f32[1024,1024]{1,0:T(8,128)S(1)}, f32[1024,1024]{1,0:T(8,128)S(1)}) custom-call(s32[6]{0:T(128)S(1)} %stack.35.flags.flag_ref, f32[256,1024]{1,0:T(8,128)S(1)} %copy-done.1, f32[256,1024]{1,0:T(8,128)S(1)} %copy-done.3, f32[256,1024]{1,0:T(8,128)} %collective-permute-done.27.refs_2_, ...), custom_call_target="tpu_custom_call", output_to_operand_aliasing={{0}: (7, {}), {1}: (8, {})} | custom-call | flops 3221225472 | bytes 1048576 | tf_op jit(solution)/shard_map/pallas_call | solution.py:45
  124.2 3.1 %collective-permute-start.15 = (f32[96,1024]{1,0:T(8,128)S(1)}, f32[96,1024]{1,0:T(8,128)S(1)}, u32[]{:S(2)}, u32[]{:S(2)}) collective-permute-start(f32[96,1024]{1,0:T(8,128)S(1)} %collective-permute-done.4.refs_1_), channel_id=1, source_target_pairs={{0,16},{3,19},{4,20},{7,23},{8,24},{11,27},{12,28},{15,31},{16,0},... | collective-permute-start | bytes 1179656 | tf_op jit(solution)/shard_map/ppermute | solution.py:200
  127.4 0.7 collective-permute-start.10
  128.1 5.8 %shard_map.36 = (f32[1024,1024]{1,0:T(8,128)S(1)}, f32[1024,1024]{1,0:T(8,128)S(1)}) custom-call(s32[6]{0:T(128)S(1)} %stack.35.flags.flag_ref, f32[256,1024]{1,0:T(8,128)S(1)} %collective-permute-done.x.refs_0_.refs_4_, f32[256,1024]{1,0:T(8,128)} %collective-permute-done.22.refs_1_, ...), custom_call_target="tpu_custom_call", output_to_operand_aliasing={{0}: (7, {}), {1}: (8, {})} | custom-call | flops 3221225472 | bytes 1048576 | tf_op jit(solution)/shard_map/pallas_call | solution.py:45
  133.9 5.5 %shard_map.37 = (f32[1024,1024]{1,0:T(8,128)S(1)}, f32[1024,1024]{1,0:T(8,128)S(1)}) custom-call(s32[6]{0:T(128)S(1)} %stack.35.flags.flag_ref, f32[256,1024]{1,0:T(8,128)S(1)} %get-tuple-element.20.refs_0_.refs_4_, f32[256,1024]{1,0:T(8,128)S(1)} %collective-permute-done.17.refs_1_, ...), custom_call_target="tpu_custom_call", output_to_operand_aliasing={{0}: (9, {}), {1}: (10, {})} | custom-call | flops 3221225472 | bytes 1048576 | tf_op jit(solution)/shard_map/pallas_call | solution.py:45
  139.4 5.5 %shard_map.38 = f32[1024,2048]{1,0:T(8,128)} custom-call(s32[6]{0:T(128)S(1)} %stack.35.flags.flag_ref, f32[160,1024]{1,0:T(8,128)S(1)} %shard_map.30.refs_0_.refs_8_, f32[96,1024]{1,0:T(8,128)S(1)} %shard_map.31.refs_1_.refs_9_, f32[160,1024]{1,0:T(8,128)S(1)} %collective-permute-done.5.refs_2_, f32[96,1024]{1,0:T(8,128)S(1)} %collective-permute-done.6.refs_3_, ...), custom_call_target="tpu_custom_call" | custom-call | flops 3221225472 | bytes 1048576 | tf_op jit(solution)/shard_map/pallas_call | solution.py:45
  (34 shorter events, 0.2 us)
Async XLA Ops:
  0.0 8.6 %collective-permute-start.11 = (f32[256,1024]{1,0:T(8,128)}, f32[256,1024]{1,0:T(8,128)S(1)}, u32[]{:S(2)}, u32[]{:S(2)}) collective-permute-start(f32[256,1024]{1,0:T(8,128)} %refs_4_.1), channel_id=1, source_target_pairs={{1,2},{2,1},{5,6},{6,5},{9,10},{10,9},{13,14},{14,13},{17,18},{18,... | collective-permute-start | bytes 3145736 | tf_op jit(solution)/shard_map/ppermute | solution.py:200
  0.7 24.5 %collective-permute-start = (f32[256,1024]{1,0:T(8,128)}, f32[256,1024]{1,0:T(8,128)S(1)}, u32[]{:S(2)}, u32[]{:S(2)}) collective-permute-start(f32[256,1024]{1,0:T(8,128)} %refs_4_.1), channel_id=1, source_target_pairs={{0,1},{1,0},{2,3},{3,2},{4,5},{5,4},{6,7},{7,6},{8,9},{9,8},{10,11... | collective-permute-start | bytes 3145736 | tf_op jit(solution)/shard_map/ppermute | solution.py:200
  2.3 23.7 %collective-permute-start.27 = (f32[256,1024]{1,0:T(8,128)}, f32[256,1024]{1,0:T(8,128)}, u32[]{:S(2)}, u32[]{:S(2)}) collective-permute-start(f32[256,1024]{1,0:T(8,128)} %refs_4_.1), channel_id=1, source_target_pairs={{0,8},{5,13},{10,2},{15,7},{16,24},{21,29},{26,18},{31,23}} | collective-permute-start | bytes 3145736 | tf_op jit(solution)/shard_map/ppermute | solution.py:200
  5.4 25.3 %collective-permute-start.20 = (f32[256,1024]{1,0:T(8,128)}, f32[256,1024]{1,0:T(8,128)}, u32[]{:S(2)}, u32[]{:S(2)}) collective-permute-start(f32[256,1024]{1,0:T(8,128)} %refs_4_.1), channel_id=1, source_target_pairs={{0,16},{1,17},{2,18},{3,19},{4,20},{5,21},{6,22},{7,23},{8,24},{9,... | collective-permute-start | bytes 3145736 | tf_op jit(solution)/shard_map/ppermute | solution.py:200
  6.6 27.0 %collective-permute-start.26 = (f32[256,1024]{1,0:T(8,128)}, f32[256,1024]{1,0:T(8,128)S(1)}, u32[]{:S(2)}, u32[]{:S(2)}) collective-permute-start(f32[256,1024]{1,0:T(8,128)} %refs_4_.1), channel_id=1, source_target_pairs={{0,4},{5,1},{10,14},{15,11},{16,20},{21,17},{26,30},{31,27}} | collective-permute-start | bytes 3145736 | tf_op jit(solution)/shard_map/ppermute | solution.py:200
  8.6 54.1 %copy-start.4 = (f32[256,1024]{1,0:T(8,128)}, f32[256,1024]{1,0:T(8,128)S(1)}, u32[]{:S(2)}) copy-start(f32[256,1024]{1,0:T(8,128)S(1)} %collective-permute-done.11.refs_1_) | copy-start | bytes 3145732
  8.7 54.1 %collective-permute-start.12 = (f32[256,1024]{1,0:T(8,128)S(1)}, f32[256,1024]{1,0:T(8,128)S(1)}, u32[]{:S(2)}, u32[]{:S(2)}) collective-permute-start(f32[256,1024]{1,0:T(8,128)S(1)} %collective-permute-done.11.refs_1_), channel_id=1, source_target_pairs={{1,0},{2,3},{5,4},{6,7},{9,8},{10,11},{13,12},{14,15},{17,16},{18,... | collective-permute-start | bytes 3145736 | tf_op jit(solution)/shard_map/ppermute | solution.py:200
  25.3 12.7 %collective-permute-start.1 = (f32[160,1024]{1,0:T(8,128)S(1)}, f32[160,1024]{1,0:T(8,128)S(1)}, u32[]{:S(2)}, u32[]{:S(2)}) collective-permute-start(f32[160,1024]{1,0:T(8,128)S(1)} %get-tuple-element.17), channel_id=1, source_target_pairs={{1,2},{2,1},{5,6},{6,5},{9,10},{10,9},{13,14},{14,13},{17,18},{18,... | collective-permute-start | bytes 1966088 | tf_op jit(solution)/shard_map/ppermute | solution.py:200
  26.0 6.3 %collective-permute-start.3 = (f32[96,1024]{1,0:T(8,128)S(1)}, f32[96,1024]{1,0:T(8,128)S(1)}, u32[]{:S(2)}, u32[]{:S(2)}) collective-permute-start(f32[96,1024]{1,0:T(8,128)S(1)} %get-tuple-element.18), channel_id=1, source_target_pairs={{1,2},{2,1},{5,6},{6,5},{9,10},{10,9},{13,14},{14,13},{17,18},{18,... | collective-permute-start | bytes 1179656 | tf_op jit(solution)/shard_map/ppermute | solution.py:200
  30.7 35.7 %collective-permute-start.28 = (f32[256,1024]{1,0:T(8,128)}, f32[256,1024]{1,0:T(8,128)}, u32[]{:S(2)}, u32[]{:S(2)}) collective-permute-start(f32[256,1024]{1,0:T(8,128)} %collective-permute-done.27.refs_2_), channel_id=1, source_target_pairs={{2,6},{7,3},{8,12},{13,9},{18,22},{23,19},{24,28},{29,25}} | collective-permute-start | bytes 3145736 | tf_op jit(solution)/shard_map/ppermute | solution.py:200
  32.3 29.2 %collective-permute-start.4 = (f32[96,1024]{1,0:T(8,128)S(1)}, f32[96,1024]{1,0:T(8,128)S(1)}, u32[]{:S(2)}, u32[]{:S(2)}) collective-permute-start(f32[96,1024]{1,0:T(8,128)S(1)} %collective-permute-done.3.refs_0_), channel_id=1, source_target_pairs={{1,0},{2,3},{5,4},{6,7},{9,8},{10,11},{13,12},{14,15},{17,16},{18,... | collective-permute-start | bytes 1179656 | tf_op jit(solution)/shard_map/ppermute | solution.py:200
  33.6 1.1 copy-start.2
  34.7 34.7 %collective-permute-start.23 = (f32[256,1024]{1,0:T(8,128)S(1)}, f32[256,1024]{1,0:T(8,128)}, u32[]{:S(2)}, u32[]{:S(2)}) collective-permute-start(f32[256,1024]{1,0:T(8,128)S(1)} %collective-permute-done.x.refs_0_.refs_4_), channel_id=1, source_target_pairs={{0,8},{5,13},{10,2},{15,7},{16,24},{21,29},{26,18},{31,23}} | collective-permute-start | bytes 3145736 | tf_op jit(solution)/shard_map/ppermute | solution.py:200
  37.9 32.8 %collective-permute-start.22 = (f32[256,1024]{1,0:T(8,128)S(1)}, f32[256,1024]{1,0:T(8,128)}, u32[]{:S(2)}, u32[]{:S(2)}) collective-permute-start(f32[256,1024]{1,0:T(8,128)S(1)} %collective-permute-done.x.refs_0_.refs_4_), channel_id=1, source_target_pairs={{0,4},{5,1},{10,14},{15,11},{16,20},{21,17},{26,30},{31,27}} | collective-permute-start | bytes 3145736 | tf_op jit(solution)/shard_map/ppermute | solution.py:200
  61.5 22.0 %collective-permute-start.25 = (f32[256,1024]{1,0:T(8,128)S(1)}, f32[256,1024]{1,0:T(8,128)}, u32[]{:S(2)}, u32[]{:S(2)}) collective-permute-start(f32[256,1024]{1,0:T(8,128)S(1)} %collective-permute-done.x.refs_0_.refs_4_), channel_id=1, source_target_pairs={{0,16},{1,17},{2,18},{3,19},{4,20},{5,21},{6,22},{7,23},{8,24},{9,... | collective-permute-start | bytes 3145736 | tf_op jit(solution)/shard_map/ppermute | solution.py:200
  62.7 26.4 %collective-permute-start.21 = (f32[256,1024]{1,0:T(8,128)}, f32[256,1024]{1,0:T(8,128)}, u32[]{:S(2)}, u32[]{:S(2)}) collective-permute-start(f32[256,1024]{1,0:T(8,128)} %collective-permute-done.20.refs_5_), channel_id=1, source_target_pairs={{1,2},{2,1},{5,6},{6,5},{9,10},{10,9},{13,14},{14,13},{17,18},{18,... | collective-permute-start | bytes 3145736 | tf_op jit(solution)/shard_map/ppermute | solution.py:200
  64.5 1.2 copy-start.5
  65.7 37.1 %copy-start = (f32[1,1,1024,2048]{3,2,1,0:T(8,128)S(1)}, f32[1,1,1024,2048]{3,2,1,0:T(8,128)}, u32[]{:S(2)}) copy-start(f32[1,1,1024,2048]{3,2,1,0:T(8,128)} %param.3) | copy-start | bytes 25165828
  66.4 26.4 %collective-permute-start.18 = (f32[256,1024]{1,0:T(8,128)S(1)}, f32[256,1024]{1,0:T(8,128)S(1)}, u32[]{:S(2)}, u32[]{:S(2)}) collective-permute-start(f32[256,1024]{1,0:T(8,128)S(1)} %get-tuple-element.20.refs_0_.refs_4_), channel_id=1, source_target_pairs={{0,8},{5,13},{10,2},{15,7},{16,24},{21,29},{26,18},{31,23}} | collective-permute-start | bytes 3145736 | tf_op jit(solution)/shard_map/ppermute | solution.py:200
  69.4 21.0 %collective-permute-start.8 = (f32[96,1024]{1,0:T(8,128)S(1)}, f32[96,1024]{1,0:T(8,128)S(1)}, u32[]{:S(2)}, u32[]{:S(2)}) collective-permute-start(f32[96,1024]{1,0:T(8,128)S(1)} %shard_map.31.refs_1_.refs_9_), channel_id=1, source_target_pairs={{0,8},{5,13},{10,2},{15,7},{16,24},{21,29},{26,18},{31,23}} | collective-permute-start | bytes 1179656 | tf_op jit(solution)/shard_map/ppermute | solution.py:200
  70.8 20.4 %collective-permute-start.2 = (f32[160,1024]{1,0:T(8,128)S(1)}, f32[160,1024]{1,0:T(8,128)S(1)}, u32[]{:S(2)}, u32[]{:S(2)}) collective-permute-start(f32[160,1024]{1,0:T(8,128)S(1)} %collective-permute-done.1.refs_0_), channel_id=1, source_target_pairs={{1,0},{2,3},{5,4},{6,7},{9,8},{10,11},{13,12},{14,15},{17,16},{18,... | collective-permute-start | bytes 1966088 | tf_op jit(solution)/shard_map/ppermute | solution.py:200
  83.5 11.2 %collective-permute-start.6 = (f32[96,1024]{1,0:T(8,128)S(1)}, f32[96,1024]{1,0:T(8,128)S(1)}, u32[]{:S(2)}, u32[]{:S(2)}) collective-permute-start(f32[96,1024]{1,0:T(8,128)S(1)} %shard_map.31.refs_1_.refs_9_), channel_id=1, source_target_pairs={{0,4},{5,1},{10,14},{15,11},{16,20},{21,17},{26,30},{31,27}} | collective-permute-start | bytes 1179656 | tf_op jit(solution)/shard_map/ppermute | solution.py:200
  89.1 11.2 %collective-permute-start.16 = (f32[96,1024]{1,0:T(8,128)S(1)}, f32[96,1024]{1,0:T(8,128)S(1)}, u32[]{:S(2)}, u32[]{:S(2)}) collective-permute-start(f32[96,1024]{1,0:T(8,128)S(1)} %get-tuple-element.19), channel_id=1, source_target_pairs={{0,16},{1,17},{2,18},{3,19},{4,20},{5,21},{6,22},{7,23},{8,24},{9,... | collective-permute-start | bytes 1179656 | tf_op jit(solution)/shard_map/ppermute | solution.py:200
  90.4 27.3 %collective-permute-start.24 = (f32[256,1024]{1,0:T(8,128)}, f32[256,1024]{1,0:T(8,128)S(1)}, u32[]{:S(2)}, u32[]{:S(2)}) collective-permute-start(f32[256,1024]{1,0:T(8,128)} %collective-permute-done.23.refs_2_), channel_id=1, source_target_pairs={{2,6},{7,3},{8,12},{13,9},{18,22},{23,19},{24,28},{29,25}} | collective-permute-start | bytes 3145736 | tf_op jit(solution)/shard_map/ppermute | solution.py:200
  91.1 33.1 %collective-permute-start.17 = (f32[256,1024]{1,0:T(8,128)S(1)}, f32[256,1024]{1,0:T(8,128)S(1)}, u32[]{:S(2)}, u32[]{:S(2)}) collective-permute-start(f32[256,1024]{1,0:T(8,128)S(1)} %get-tuple-element.20.refs_0_.refs_4_), channel_id=1, source_target_pairs={{0,4},{5,1},{10,14},{15,11},{16,20},{21,17},{26,30},{31,27}} | collective-permute-start | bytes 3145736 | tf_op jit(solution)/shard_map/ppermute | solution.py:200
  92.8 34.6 %collective-permute-start.19 = (f32[256,1024]{1,0:T(8,128)S(1)}, f32[256,1024]{1,0:T(8,128)S(1)}, u32[]{:S(2)}, u32[]{:S(2)}) collective-permute-start(f32[256,1024]{1,0:T(8,128)S(1)} %collective-permute-done.18.refs_2_), channel_id=1, source_target_pairs={{2,6},{7,3},{8,12},{13,9},{18,22},{23,19},{24,28},{29,25}} | collective-permute-start | bytes 3145736 | tf_op jit(solution)/shard_map/ppermute | solution.py:200
  94.7 19.3 %collective-permute-start.13 = (f32[160,1024]{1,0:T(8,128)S(1)}, f32[160,1024]{1,0:T(8,128)S(1)}, u32[]{:S(2)}, u32[]{:S(2)}) collective-permute-start(f32[160,1024]{1,0:T(8,128)S(1)} %shard_map.32), channel_id=1, source_target_pairs={{0,16},{1,17},{2,18},{3,19},{4,20},{5,21},{6,22},{7,23},{8,24},{9,... | collective-permute-start | bytes 1966088 | tf_op jit(solution)/shard_map/ppermute | solution.py:200
  100.3 16.0 %collective-permute-start.7 = (f32[160,1024]{1,0:T(8,128)S(1)}, f32[160,1024]{1,0:T(8,128)S(1)}, u32[]{:S(2)}, u32[]{:S(2)}) collective-permute-start(f32[160,1024]{1,0:T(8,128)S(1)} %shard_map.30.refs_0_.refs_8_), channel_id=1, source_target_pairs={{0,8},{5,13},{10,2},{15,7},{16,24},{21,29},{26,18},{31,23}} | collective-permute-start | bytes 1966088 | tf_op jit(solution)/shard_map/ppermute | solution.py:200
  102.8 15.6 %copy-start.1 = (f32[256,1024]{1,0:T(8,128)S(1)}, f32[256,1024]{1,0:T(8,128)}, u32[]{:S(2)}) copy-start(f32[256,1024]{1,0:T(8,128)} %refs_4_.1) | copy-start | bytes 3145732
  102.8 15.6 %copy-start.3 = (f32[256,1024]{1,0:T(8,128)S(1)}, f32[256,1024]{1,0:T(8,128)}, u32[]{:S(2)}) copy-start(f32[256,1024]{1,0:T(8,128)} %copy-done.2) | copy-start | bytes 3145732
  114.0 25.3 %collective-permute-start.5 = (f32[160,1024]{1,0:T(8,128)S(1)}, f32[160,1024]{1,0:T(8,128)S(1)}, u32[]{:S(2)}, u32[]{:S(2)}) collective-permute-start(f32[160,1024]{1,0:T(8,128)S(1)} %shard_map.30.refs_0_.refs_8_), channel_id=1, source_target_pairs={{0,4},{5,1},{10,14},{15,11},{16,20},{21,17},{26,30},{31,27}} | collective-permute-start | bytes 1966088 | tf_op jit(solution)/shard_map/ppermute | solution.py:200
  116.4 23.0 %collective-permute-start.14 = (f32[160,1024]{1,0:T(8,128)S(1)}, f32[160,1024]{1,0:T(8,128)S(1)}, u32[]{:S(2)}, u32[]{:S(2)}) collective-permute-start(f32[160,1024]{1,0:T(8,128)S(1)} %collective-permute-done.13.refs_5_.refs_11_), channel_id=1, source_target_pairs={{1,0},{2,3},{5,4},{6,7},{9,8},{10,11},{13,12},{14,15},{17,16},{18,... | collective-permute-start | bytes 1966088 | tf_op jit(solution)/shard_map/ppermute | solution.py:200
  117.7 21.7 %collective-permute-start.9 = (f32[160,1024]{1,0:T(8,128)S(1)}, f32[160,1024]{1,0:T(8,128)S(1)}, u32[]{:S(2)}, u32[]{:S(2)}) collective-permute-start(f32[160,1024]{1,0:T(8,128)S(1)} %collective-permute-done.7.refs_4_), channel_id=1, source_target_pairs={{2,6},{7,3},{8,12},{13,9},{18,22},{23,19},{24,28},{29,25}} | collective-permute-start | bytes 1966088 | tf_op jit(solution)/shard_map/ppermute | solution.py:200
  124.2 15.1 %collective-permute-start.15 = (f32[96,1024]{1,0:T(8,128)S(1)}, f32[96,1024]{1,0:T(8,128)S(1)}, u32[]{:S(2)}, u32[]{:S(2)}) collective-permute-start(f32[96,1024]{1,0:T(8,128)S(1)} %collective-permute-done.4.refs_1_), channel_id=1, source_target_pairs={{0,16},{3,19},{4,20},{7,23},{8,24},{11,27},{12,28},{15,31},{16,0},... | collective-permute-start | bytes 1179656 | tf_op jit(solution)/shard_map/ppermute | solution.py:200
  127.4 12.0 %collective-permute-start.10 = (f32[96,1024]{1,0:T(8,128)S(1)}, f32[96,1024]{1,0:T(8,128)S(1)}, u32[]{:S(2)}, u32[]{:S(2)}) collective-permute-start(f32[96,1024]{1,0:T(8,128)S(1)} %collective-permute-done.8.refs_5_), channel_id=1, source_target_pairs={{2,6},{7,3},{8,12},{13,9},{18,22},{23,19},{24,28},{29,25}} | collective-permute-start | bytes 1179656 | tf_op jit(solution)/shard_map/ppermute | solution.py:200

commit v3 on v2

--- a/solution.py
+++ b/solution.py
@@ -68,10 +68,6 @@
         copy.wait()
 
 
-def mark(flags, out):
-    out[...] = jnp.full(out.shape, flags[0])
-
-
 def part(x, first, second):
     at = first.shape[0]
     first[...] = x[:at]
@@ -153,7 +149,7 @@
     return call(kernel, args, outs, {first + i: i for i in range(n)}, scratch, flops=flops, mib=SUM_MIB)
 
 
-def finish(flags, left, rights, accs, halves, shape, tile=128):
+def finish(flags, left, rights, accs, halves, shape, tile=256):
     operands = [left, *rights]
     arrays = [a for p in operands for a in p.arrays]
     height, width = accs[0].shape
@@ -228,26 +224,25 @@
     f0 = send(y0, beyond)
 
     a2 = send(b1, outward)
-    call(mark, [(flags, SMEM)], [(pltpu.VMEM((8, 128), jnp.int32), VMEM)], mib=1)
     parts = [(pltpu.VMEM((n, width), F32), VMEM) for n in (cut, depth - cut)]
     p1a, p1b = call(part, [(a1, VMEM)], parts, mib=8)
     b2a = send(p1a, middle)
     x2 = send(a1, swap)
+    y1 = send(a1, across)
     b2b = send(p1b, middle)
-    y1 = send(a1, across)
     e1 = send(a1, beside)
-    b3 = send(x1, middle)
     left = Operand((PLACE, (panel, e0, y0, f0)))
     own, other = accumulate(flags, left, [Operand(panel), Operand(x1)], [own, other])
 
     a3a = send(b2a, outward)
     f1 = send(y1, beyond)
-    (s3a,) = select(INNER, flags, [b2a], [a2])
+    b3 = send(x1, middle)
+    s3a, p2 = select(INNER, flags, [b2a, b1], [a2, a2])
     x3a = send(s3a, swap)
+    y2 = send(p2, across)
     a3b = send(b2b, outward)
-    s3b, p2 = select(INNER, flags, [b2b, b1], [(a2, cut), a2])
+    (s3b,) = select(INNER, flags, [b2b], [(a2, cut)])
     x3b = send(s3b, swap)
-    y2 = send(p2, across)
     e2 = send(p2, beside)
     left = Operand((PLACE, (a1, e1, y1, f1)))
     own, other = accumulate(flags, left, [Operand(a1), Operand(x2)], [own, other])

time: 146 us -> 146 us (level)
  waiting for transfers between devices: 65.8 us -> 67.5 us
    ppermute x29, waiting for transfers between devices: 65.8 us -> 67.5 us  [send(): return lax.ppermute(x, AXES, pairs)]
    pallas_call x11 -> x10, Pallas kernels: 28.8 us -> 27.6 us  [call(): pl.pallas_call(kernel, in_specs=[spec for _, spec in args], out_specs=[sp...]
  transfers between devices with their start and end apart: 29 -> 29, of which waited for: 6 -> 6; matrix products, arithmetic and copies ran while one was open for 0% -> 0% of each run, Pallas kernels for 16% -> 15%
where the time goes in v3:
time: 146 us
  waiting for transfers between devices  67.5 us (46%)
  starting transfers between devices  47.4 us (32%)
  Pallas kernels  27.6 us (19%)
  local copies, waits for them, and re-layouts  2.4 us (2%)
    ppermute x29, waiting for transfers between devices, send(): return lax.ppermute(x, AXES, pairs)  67.5 us
    ppermute x29, starting transfers between devices, send(): return lax.ppermute(x, AXES, pairs)  47.4 us
    pallas_call x10, Pallas kernels, call(): pl.pallas_call(kernel, in_specs=[spec for _, spec in args], out_specs=[sp...  27.6 us
  transfers between devices with their start and end apart: 29, of which 6 were waited for; matrix products, arithmetic and copies ran while one was open for 0% of the time, Pallas kernels for 15%

profile of v3, /device:TPU:29, one launch (start us, length us, event | category | flops | bytes accessed | tf_op | source)
XLA Modules:
  0.0 145.6 jit_solution(11048044555756015754)
XLA Ops:
  0.0 0.7 collective-permute-start.11
  0.7 1.6 %collective-permute-start = (f32[256,1024]{1,0:T(8,128)}, f32[256,1024]{1,0:T(8,128)S(1)}, u32[]{:S(2)}, u32[]{:S(2)}) collective-permute-start(f32[256,1024]{1,0:T(8,128)} %refs_4_.1), channel_id=1, source_target_pairs={{0,1},{1,0},{2,3},{3,2},{4,5},{5,4},{6,7},{7,6},{8,9},{9,8},{10,11... | collective-permute-start | bytes 3145736 | tf_op jit(solution)/shard_map/ppermute | solution.py:196
  2.3 3.1 %collective-permute-start.27 = (f32[256,1024]{1,0:T(8,128)}, f32[256,1024]{1,0:T(8,128)}, u32[]{:S(2)}, u32[]{:S(2)}) collective-permute-start(f32[256,1024]{1,0:T(8,128)} %refs_4_.1), channel_id=1, source_target_pairs={{0,8},{5,13},{10,2},{15,7},{16,24},{21,29},{26,18},{31,23}} | collective-permute-start | bytes 3145736 | tf_op jit(solution)/shard_map/ppermute | solution.py:196
  5.4 1.2 collective-permute-start.20
  6.6 2.0 %collective-permute-start.26 = (f32[256,1024]{1,0:T(8,128)}, f32[256,1024]{1,0:T(8,128)S(1)}, u32[]{:S(2)}, u32[]{:S(2)}) collective-permute-start(f32[256,1024]{1,0:T(8,128)} %refs_4_.1), channel_id=1, source_target_pairs={{0,4},{5,1},{10,14},{15,11},{16,20},{21,17},{26,30},{31,27}} | collective-permute-start | bytes 3145736 | tf_op jit(solution)/shard_map/ppermute | solution.py:196
  8.7 1.3 collective-permute-start.12
  10.0 15.3 %collective-permute-done.x.refs_0_.refs_4_ = f32[256,1024]{1,0:T(8,128)S(1)} collective-permute-done((f32[256,1024]{1,0:T(8,128)}, f32[256,1024]{1,0:T(8,128)S(1)}, u32[]{:S(2)}, u32[]{:S(2)}) %collective-permute-start) | collective-permute-done | bytes 1048608 | tf_op jit(solution)/shard_map/ppermute | solution.py:196
  25.2 0.1 shard_map.28
  25.3 0.7 collective-permute-start.1
  26.0 0.7 collective-permute-start.3
  26.7 4.0 %collective-permute-done.20.refs_5_ = f32[256,1024]{1,0:T(8,128)} collective-permute-done((f32[256,1024]{1,0:T(8,128)}, f32[256,1024]{1,0:T(8,128)}, u32[]{:S(2)}, u32[]{:S(2)}) %collective-permute-start.20) | collective-permute-done | bytes 1048608 | tf_op jit(solution)/shard_map/ppermute | solution.py:196
  30.7 1.6 %collective-permute-start.28 = (f32[256,1024]{1,0:T(8,128)}, f32[256,1024]{1,0:T(8,128)}, u32[]{:S(2)}, u32[]{:S(2)}) collective-permute-start(f32[256,1024]{1,0:T(8,128)} %collective-permute-done.27.refs_2_), channel_id=1, source_target_pairs={{2,6},{7,3},{8,12},{13,9},{18,22},{23,19},{24,28},{29,25}} | collective-permute-start | bytes 3145736 | tf_op jit(solution)/shard_map/ppermute | solution.py:196
  32.3 1.3 collective-permute-start.4
  33.6 1.1 copy-done.2
  34.7 3.2 %collective-permute-start.23 = (f32[256,1024]{1,0:T(8,128)S(1)}, f32[256,1024]{1,0:T(8,128)}, u32[]{:S(2)}, u32[]{:S(2)}) collective-permute-start(f32[256,1024]{1,0:T(8,128)S(1)} %collective-permute-done.x.refs_0_.refs_4_), channel_id=1, source_target_pairs={{0,8},{5,13},{10,2},{15,7},{16,24},{21,29},{26,18},{31,23}} | collective-permute-start | bytes 3145736 | tf_op jit(solution)/shard_map/ppermute | solution.py:196
  37.9 2.3 %collective-permute-start.22 = (f32[256,1024]{1,0:T(8,128)S(1)}, f32[256,1024]{1,0:T(8,128)}, u32[]{:S(2)}, u32[]{:S(2)}) collective-permute-start(f32[256,1024]{1,0:T(8,128)S(1)} %collective-permute-done.x.refs_0_.refs_4_), channel_id=1, source_target_pairs={{0,4},{5,1},{10,14},{15,11},{16,20},{21,17},{26,30},{31,27}} | collective-permute-start | bytes 3145736 | tf_op jit(solution)/shard_map/ppermute | solution.py:196
  40.2 21.3 %collective-permute-done.4.refs_1_ = f32[96,1024]{1,0:T(8,128)S(1)} collective-permute-done((f32[96,1024]{1,0:T(8,128)S(1)}, f32[96,1024]{1,0:T(8,128)S(1)}, u32[]{:S(2)}, u32[]{:S(2)}) %collective-permute-start.4) | collective-permute-done | bytes 393248 | tf_op jit(solution)/shard_map/ppermute | solution.py:196
  61.5 1.2 collective-permute-start.25
  62.7 1.7 %collective-permute-start.21 = (f32[256,1024]{1,0:T(8,128)}, f32[256,1024]{1,0:T(8,128)}, u32[]{:S(2)}, u32[]{:S(2)}) collective-permute-start(f32[256,1024]{1,0:T(8,128)} %collective-permute-done.20.refs_5_), channel_id=1, source_target_pairs={{1,2},{2,1},{5,6},{6,5},{9,10},{10,9},{13,14},{14,13},{17,18},{18,... | collective-permute-start | bytes 3145736 | tf_op jit(solution)/shard_map/ppermute | solution.py:196
  64.4 0.1 stack.35.flag_ref.flags
  64.5 1.2 copy-done.5
  65.7 0.7 shard_map.31
  66.4 2.5 %collective-permute-start.18 = (f32[256,1024]{1,0:T(8,128)S(1)}, f32[256,1024]{1,0:T(8,128)S(1)}, u32[]{:S(2)}, u32[]{:S(2)}) collective-permute-start(f32[256,1024]{1,0:T(8,128)S(1)} %get-tuple-element.20.refs_0_.refs_4_), channel_id=1, source_target_pairs={{0,8},{5,13},{10,2},{15,7},{16,24},{21,29},{26,18},{31,23}} | collective-permute-start | bytes 3145736 | tf_op jit(solution)/shard_map/ppermute | solution.py:196
  68.9 0.6 shard_map.30.refs_1_.refs_9_
  69.5 1.3 collective-permute-start.8
  70.8 1.3 collective-permute-start.2
  72.1 11.4 %collective-permute-done.25.refs_5_ = f32[256,1024]{1,0:T(8,128)} collective-permute-done((f32[256,1024]{1,0:T(8,128)S(1)}, f32[256,1024]{1,0:T(8,128)}, u32[]{:S(2)}, u32[]{:S(2)}) %collective-permute-start.25) | collective-permute-done | bytes 1048608 | tf_op jit(solution)/shard_map/ppermute | solution.py:196
  83.5 5.6 %collective-permute-start.6 = (f32[96,1024]{1,0:T(8,128)S(1)}, f32[96,1024]{1,0:T(8,128)S(1)}, u32[]{:S(2)}, u32[]{:S(2)}) collective-permute-start(f32[96,1024]{1,0:T(8,128)S(1)} %shard_map.30.refs_1_.refs_9_), channel_id=1, source_target_pairs={{0,4},{5,1},{10,14},{15,11},{16,20},{21,17},{26,30},{31,27}} | collective-permute-start | bytes 1179656 | tf_op jit(solution)/shard_map/ppermute | solution.py:196
  89.1 0.6 shard_map.32
  89.7 1.3 collective-permute-start.16
  91.0 0.7 collective-permute-start.24
  91.7 1.6 %collective-permute-start.17 = (f32[256,1024]{1,0:T(8,128)S(1)}, f32[256,1024]{1,0:T(8,128)S(1)}, u32[]{:S(2)}, u32[]{:S(2)}) collective-permute-start(f32[256,1024]{1,0:T(8,128)S(1)} %get-tuple-element.20.refs_0_.refs_4_), channel_id=1, source_target_pairs={{0,4},{5,1},{10,14},{15,11},{16,20},{21,17},{26,30},{31,27}} | collective-permute-start | bytes 3145736 | tf_op jit(solution)/shard_map/ppermute | solution.py:196
  93.4 0.7 collective-permute-start.19
  94.1 0.6 shard_map.29.refs_0_.refs_8_
  94.7 0.3 collective-permute-start.13
  95.0 5.9 %collective-permute-done.16.refs_6_.refs_13_ = f32[96,1024]{1,0:T(8,128)S(1)} collective-permute-done((f32[96,1024]{1,0:T(8,128)S(1)}, f32[96,1024]{1,0:T(8,128)S(1)}, u32[]{:S(2)}, u32[]{:S(2)}) %collective-permute-start.16) | collective-permute-done | bytes 393248 | tf_op jit(solution)/shard_map/ppermute | solution.py:196
  100.9 1.3 collective-permute-start.7
  102.3 2.6 %shard_map.33 = (f32[1024,1024]{1,0:T(8,128)S(1)}, f32[1024,1024]{1,0:T(8,128)S(1)}) custom-call(s32[6]{0:T(128)S(1)} %stack.35.flag_ref.flags, f32[1024,2048]{1,0:T(8,128)S(1)} %bitcast.8), custom_call_target="tpu_custom_call" | custom-call | flops 1048576 | bytes 1048576 | tf_op jit(solution)/shard_map/pallas_call | solution.py:45
  104.9 9.7 %collective-permute-done.13.refs_5_.refs_11_ = f32[160,1024]{1,0:T(8,128)S(1)} collective-permute-done((f32[160,1024]{1,0:T(8,128)S(1)}, f32[160,1024]{1,0:T(8,128)S(1)}, u32[]{:S(2)}, u32[]{:S(2)}) %collective-permute-start.13) | collective-permute-done | bytes 655392 | tf_op jit(solution)/shard_map/ppermute | solution.py:196
  114.6 2.3 %collective-permute-start.5 = (f32[160,1024]{1,0:T(8,128)S(1)}, f32[160,1024]{1,0:T(8,128)S(1)}, u32[]{:S(2)}, u32[]{:S(2)}) collective-permute-start(f32[160,1024]{1,0:T(8,128)S(1)} %shard_map.29.refs_0_.refs_8_), channel_id=1, source_target_pairs={{0,4},{5,1},{10,14},{15,11},{16,20},{21,17},{26,30},{31,27}} | collective-permute-start | bytes 1966088 | tf_op jit(solution)/shard_map/ppermute | solution.py:196
  117.0 1.3 collective-permute-start.14
  118.3 0.7 collective-permute-start.9
  119.0 5.8 %shard_map.34 = (f32[1024,1024]{1,0:T(8,128)S(1)}, f32[1024,1024]{1,0:T(8,128)S(1)}) custom-call(s32[6]{0:T(128)S(1)} %stack.35.flag_ref.flags, f32[256,1024]{1,0:T(8,128)S(1)} %copy-done.1, f32[256,1024]{1,0:T(8,128)S(1)} %copy-done.3, f32[256,1024]{1,0:T(8,128)} %collective-permute-done.27.refs_2_, ...), custom_call_target="tpu_custom_call", output_to_operand_aliasing={{0}: (7, {}), {1}: (8, {})} | custom-call | flops 3221225472 | bytes 1048576 | tf_op jit(solution)/shard_map/pallas_call | solution.py:45
  124.9 3.1 %collective-permute-start.15 = (f32[96,1024]{1,0:T(8,128)S(1)}, f32[96,1024]{1,0:T(8,128)S(1)}, u32[]{:S(2)}, u32[]{:S(2)}) collective-permute-start(f32[96,1024]{1,0:T(8,128)S(1)} %collective-permute-done.4.refs_1_), channel_id=1, source_target_pairs={{0,16},{3,19},{4,20},{7,23},{8,24},{11,27},{12,28},{15,31},{16,0},... | collective-permute-start | bytes 1179656 | tf_op jit(solution)/shard_map/ppermute | solution.py:196
  128.0 0.7 collective-permute-start.10
  128.6 5.8 %shard_map.35 = (f32[1024,1024]{1,0:T(8,128)S(1)}, f32[1024,1024]{1,0:T(8,128)S(1)}) custom-call(s32[6]{0:T(128)S(1)} %stack.35.flag_ref.flags, f32[256,1024]{1,0:T(8,128)S(1)} %collective-permute-done.x.refs_0_.refs_4_, f32[256,1024]{1,0:T(8,128)} %collective-permute-done.22.refs_1_, ...), custom_call_target="tpu_custom_call", output_to_operand_aliasing={{0}: (7, {}), {1}: (8, {})} | custom-call | flops 3221225472 | bytes 1048576 | tf_op jit(solution)/shard_map/pallas_call | solution.py:45
  134.5 5.4 %shard_map.36 = (f32[1024,1024]{1,0:T(8,128)S(1)}, f32[1024,1024]{1,0:T(8,128)S(1)}) custom-call(s32[6]{0:T(128)S(1)} %stack.35.flag_ref.flags, f32[256,1024]{1,0:T(8,128)S(1)} %get-tuple-element.20.refs_0_.refs_4_, f32[256,1024]{1,0:T(8,128)S(1)} %collective-permute-done.17.refs_1_, ...), custom_call_target="tpu_custom_call", output_to_operand_aliasing={{0}: (9, {}), {1}: (10, {})} | custom-call | flops 3221225472 | bytes 1048576 | tf_op jit(solution)/shard_map/pallas_call | solution.py:45
  140.0 5.4 %shard_map.37 = f32[1024,2048]{1,0:T(8,128)} custom-call(s32[6]{0:T(128)S(1)} %stack.35.flag_ref.flags, f32[160,1024]{1,0:T(8,128)S(1)} %shard_map.29.refs_0_.refs_8_, f32[96,1024]{1,0:T(8,128)S(1)} %shard_map.30.refs_1_.refs_9_, f32[160,1024]{1,0:T(8,128)S(1)} %collective-permute-done.5.refs_2_, f32[96,1024]{1,0:T(8,128)S(1)} %collective-permute-done.6.refs_3_, ...), custom_call_target="tpu_custom_call" | custom-call | flops 3221225472 | bytes 1048576 | tf_op jit(solution)/shard_map/pallas_call | solution.py:45
  (33 shorter events, 0.1 us)
Async XLA Ops:
  0.0 8.6 %collective-permute-start.11 = (f32[256,1024]{1,0:T(8,128)}, f32[256,1024]{1,0:T(8,128)S(1)}, u32[]{:S(2)}, u32[]{:S(2)}) collective-permute-start(f32[256,1024]{1,0:T(8,128)} %refs_4_.1), channel_id=1, source_target_pairs={{1,2},{2,1},{5,6},{6,5},{9,10},{10,9},{13,14},{14,13},{17,18},{18,... | collective-permute-start | bytes 3145736 | tf_op jit(solution)/shard_map/ppermute | solution.py:196
  0.7 24.5 %collective-permute-start = (f32[256,1024]{1,0:T(8,128)}, f32[256,1024]{1,0:T(8,128)S(1)}, u32[]{:S(2)}, u32[]{:S(2)}) collective-permute-start(f32[256,1024]{1,0:T(8,128)} %refs_4_.1), channel_id=1, source_target_pairs={{0,1},{1,0},{2,3},{3,2},{4,5},{5,4},{6,7},{7,6},{8,9},{9,8},{10,11... | collective-permute-start | bytes 3145736 | tf_op jit(solution)/shard_map/ppermute | solution.py:196
  2.3 23.7 %collective-permute-start.27 = (f32[256,1024]{1,0:T(8,128)}, f32[256,1024]{1,0:T(8,128)}, u32[]{:S(2)}, u32[]{:S(2)}) collective-permute-start(f32[256,1024]{1,0:T(8,128)} %refs_4_.1), channel_id=1, source_target_pairs={{0,8},{5,13},{10,2},{15,7},{16,24},{21,29},{26,18},{31,23}} | collective-permute-start | bytes 3145736 | tf_op jit(solution)/shard_map/ppermute | solution.py:196
  5.4 25.3 %collective-permute-start.20 = (f32[256,1024]{1,0:T(8,128)}, f32[256,1024]{1,0:T(8,128)}, u32[]{:S(2)}, u32[]{:S(2)}) collective-permute-start(f32[256,1024]{1,0:T(8,128)} %refs_4_.1), channel_id=1, source_target_pairs={{0,16},{1,17},{2,18},{3,19},{4,20},{5,21},{6,22},{7,23},{8,24},{9,... | collective-permute-start | bytes 3145736 | tf_op jit(solution)/shard_map/ppermute | solution.py:196
  6.6 27.0 %collective-permute-start.26 = (f32[256,1024]{1,0:T(8,128)}, f32[256,1024]{1,0:T(8,128)S(1)}, u32[]{:S(2)}, u32[]{:S(2)}) collective-permute-start(f32[256,1024]{1,0:T(8,128)} %refs_4_.1), channel_id=1, source_target_pairs={{0,4},{5,1},{10,14},{15,11},{16,20},{21,17},{26,30},{31,27}} | collective-permute-start | bytes 3145736 | tf_op jit(solution)/shard_map/ppermute | solution.py:196
  8.6 54.1 %copy-start.4 = (f32[256,1024]{1,0:T(8,128)}, f32[256,1024]{1,0:T(8,128)S(1)}, u32[]{:S(2)}) copy-start(f32[256,1024]{1,0:T(8,128)S(1)} %collective-permute-done.11.refs_1_) | copy-start | bytes 3145732
  8.7 54.1 %collective-permute-start.12 = (f32[256,1024]{1,0:T(8,128)S(1)}, f32[256,1024]{1,0:T(8,128)S(1)}, u32[]{:S(2)}, u32[]{:S(2)}) collective-permute-start(f32[256,1024]{1,0:T(8,128)S(1)} %collective-permute-done.11.refs_1_), channel_id=1, source_target_pairs={{1,0},{2,3},{5,4},{6,7},{9,8},{10,11},{13,12},{14,15},{17,16},{18,... | collective-permute-start | bytes 3145736 | tf_op jit(solution)/shard_map/ppermute | solution.py:196
  25.3 12.7 %collective-permute-start.1 = (f32[160,1024]{1,0:T(8,128)S(1)}, f32[160,1024]{1,0:T(8,128)S(1)}, u32[]{:S(2)}, u32[]{:S(2)}) collective-permute-start(f32[160,1024]{1,0:T(8,128)S(1)} %get-tuple-element.17), channel_id=1, source_target_pairs={{1,2},{2,1},{5,6},{6,5},{9,10},{10,9},{13,14},{14,13},{17,18},{18,... | collective-permute-start | bytes 1966088 | tf_op jit(solution)/shard_map/ppermute | solution.py:196
  26.0 6.3 %collective-permute-start.3 = (f32[96,1024]{1,0:T(8,128)S(1)}, f32[96,1024]{1,0:T(8,128)S(1)}, u32[]{:S(2)}, u32[]{:S(2)}) collective-permute-start(f32[96,1024]{1,0:T(8,128)S(1)} %get-tuple-element.18), channel_id=1, source_target_pairs={{1,2},{2,1},{5,6},{6,5},{9,10},{10,9},{13,14},{14,13},{17,18},{18,... | collective-permute-start | bytes 1179656 | tf_op jit(solution)/shard_map/ppermute | solution.py:196
  30.7 35.7 %collective-permute-start.28 = (f32[256,1024]{1,0:T(8,128)}, f32[256,1024]{1,0:T(8,128)}, u32[]{:S(2)}, u32[]{:S(2)}) collective-permute-start(f32[256,1024]{1,0:T(8,128)} %collective-permute-done.27.refs_2_), channel_id=1, source_target_pairs={{2,6},{7,3},{8,12},{13,9},{18,22},{23,19},{24,28},{29,25}} | collective-permute-start | bytes 3145736 | tf_op jit(solution)/shard_map/ppermute | solution.py:196
  32.3 29.2 %collective-permute-start.4 = (f32[96,1024]{1,0:T(8,128)S(1)}, f32[96,1024]{1,0:T(8,128)S(1)}, u32[]{:S(2)}, u32[]{:S(2)}) collective-permute-start(f32[96,1024]{1,0:T(8,128)S(1)} %collective-permute-done.3.refs_0_), channel_id=1, source_target_pairs={{1,0},{2,3},{5,4},{6,7},{9,8},{10,11},{13,12},{14,15},{17,16},{18,... | collective-permute-start | bytes 1179656 | tf_op jit(solution)/shard_map/ppermute | solution.py:196
  33.6 1.1 copy-start.2
  34.7 34.8 %collective-permute-start.23 = (f32[256,1024]{1,0:T(8,128)S(1)}, f32[256,1024]{1,0:T(8,128)}, u32[]{:S(2)}, u32[]{:S(2)}) collective-permute-start(f32[256,1024]{1,0:T(8,128)S(1)} %collective-permute-done.x.refs_0_.refs_4_), channel_id=1, source_target_pairs={{0,8},{5,13},{10,2},{15,7},{16,24},{21,29},{26,18},{31,23}} | collective-permute-start | bytes 3145736 | tf_op jit(solution)/shard_map/ppermute | solution.py:196
  37.9 32.8 %collective-permute-start.22 = (f32[256,1024]{1,0:T(8,128)S(1)}, f32[256,1024]{1,0:T(8,128)}, u32[]{:S(2)}, u32[]{:S(2)}) collective-permute-start(f32[256,1024]{1,0:T(8,128)S(1)} %collective-permute-done.x.refs_0_.refs_4_), channel_id=1, source_target_pairs={{0,4},{5,1},{10,14},{15,11},{16,20},{21,17},{26,30},{31,27}} | collective-permute-start | bytes 3145736 | tf_op jit(solution)/shard_map/ppermute | solution.py:196
  61.5 22.0 %collective-permute-start.25 = (f32[256,1024]{1,0:T(8,128)S(1)}, f32[256,1024]{1,0:T(8,128)}, u32[]{:S(2)}, u32[]{:S(2)}) collective-permute-start(f32[256,1024]{1,0:T(8,128)S(1)} %collective-permute-done.x.refs_0_.refs_4_), channel_id=1, source_target_pairs={{0,16},{1,17},{2,18},{3,19},{4,20},{5,21},{6,22},{7,23},{8,24},{9,... | collective-permute-start | bytes 3145736 | tf_op jit(solution)/shard_map/ppermute | solution.py:196
  62.7 27.0 %collective-permute-start.21 = (f32[256,1024]{1,0:T(8,128)}, f32[256,1024]{1,0:T(8,128)}, u32[]{:S(2)}, u32[]{:S(2)}) collective-permute-start(f32[256,1024]{1,0:T(8,128)} %collective-permute-done.20.refs_5_), channel_id=1, source_target_pairs={{1,2},{2,1},{5,6},{6,5},{9,10},{10,9},{13,14},{14,13},{17,18},{18,... | collective-permute-start | bytes 3145736 | tf_op jit(solution)/shard_map/ppermute | solution.py:196
  64.5 1.2 copy-start.5
  65.7 36.5 %copy-start = (f32[1,1,1024,2048]{3,2,1,0:T(8,128)S(1)}, f32[1,1,1024,2048]{3,2,1,0:T(8,128)}, u32[]{:S(2)}) copy-start(f32[1,1,1024,2048]{3,2,1,0:T(8,128)} %param.3) | copy-start | bytes 25165828
  66.4 27.0 %collective-permute-start.18 = (f32[256,1024]{1,0:T(8,128)S(1)}, f32[256,1024]{1,0:T(8,128)S(1)}, u32[]{:S(2)}, u32[]{:S(2)}) collective-permute-start(f32[256,1024]{1,0:T(8,128)S(1)} %get-tuple-element.20.refs_0_.refs_4_), channel_id=1, source_target_pairs={{0,8},{5,13},{10,2},{15,7},{16,24},{21,29},{26,18},{31,23}} | collective-permute-start | bytes 3145736 | tf_op jit(solution)/shard_map/ppermute | solution.py:196
  69.5 21.5 %collective-permute-start.8 = (f32[96,1024]{1,0:T(8,128)S(1)}, f32[96,1024]{1,0:T(8,128)S(1)}, u32[]{:S(2)}, u32[]{:S(2)}) collective-permute-start(f32[96,1024]{1,0:T(8,128)S(1)} %shard_map.30.refs_1_.refs_9_), channel_id=1, source_target_pairs={{0,8},{5,13},{10,2},{15,7},{16,24},{21,29},{26,18},{31,23}} | collective-permute-start | bytes 1179656 | tf_op jit(solution)/shard_map/ppermute | solution.py:196
  70.8 20.9 %collective-permute-start.2 = (f32[160,1024]{1,0:T(8,128)S(1)}, f32[160,1024]{1,0:T(8,128)S(1)}, u32[]{:S(2)}, u32[]{:S(2)}) collective-permute-start(f32[160,1024]{1,0:T(8,128)S(1)} %collective-permute-done.1.refs_0_), channel_id=1, source_target_pairs={{1,0},{2,3},{5,4},{6,7},{9,8},{10,11},{13,12},{14,15},{17,16},{18,... | collective-permute-start | bytes 1966088 | tf_op jit(solution)/shard_map/ppermute | solution.py:196
  83.5 11.2 %collective-permute-start.6 = (f32[96,1024]{1,0:T(8,128)S(1)}, f32[96,1024]{1,0:T(8,128)S(1)}, u32[]{:S(2)}, u32[]{:S(2)}) collective-permute-start(f32[96,1024]{1,0:T(8,128)S(1)} %shard_map.30.refs_1_.refs_9_), channel_id=1, source_target_pairs={{0,4},{5,1},{10,14},{15,11},{16,20},{21,17},{26,30},{31,27}} | collective-permute-start | bytes 1179656 | tf_op jit(solution)/shard_map/ppermute | solution.py:196
  89.7 11.2 %collective-permute-start.16 = (f32[96,1024]{1,0:T(8,128)S(1)}, f32[96,1024]{1,0:T(8,128)S(1)}, u32[]{:S(2)}, u32[]{:S(2)}) collective-permute-start(f32[96,1024]{1,0:T(8,128)S(1)} %shard_map.32), channel_id=1, source_target_pairs={{0,16},{1,17},{2,18},{3,19},{4,20},{5,21},{6,22},{7,23},{8,24},{9,... | collective-permute-start | bytes 1179656 | tf_op jit(solution)/shard_map/ppermute | solution.py:196
  91.0 27.3 %collective-permute-start.24 = (f32[256,1024]{1,0:T(8,128)}, f32[256,1024]{1,0:T(8,128)S(1)}, u32[]{:S(2)}, u32[]{:S(2)}) collective-permute-start(f32[256,1024]{1,0:T(8,128)} %collective-permute-done.23.refs_2_), channel_id=1, source_target_pairs={{2,6},{7,3},{8,12},{13,9},{18,22},{23,19},{24,28},{29,25}} | collective-permute-start | bytes 3145736 | tf_op jit(solution)/shard_map/ppermute | solution.py:196
  91.7 33.1 %collective-permute-start.17 = (f32[256,1024]{1,0:T(8,128)S(1)}, f32[256,1024]{1,0:T(8,128)S(1)}, u32[]{:S(2)}, u32[]{:S(2)}) collective-permute-start(f32[256,1024]{1,0:T(8,128)S(1)} %get-tuple-element.20.refs_0_.refs_4_), channel_id=1, source_target_pairs={{0,4},{5,1},{10,14},{15,11},{16,20},{21,17},{26,30},{31,27}} | collective-permute-start | bytes 3145736 | tf_op jit(solution)/shard_map/ppermute | solution.py:196
  93.4 34.6 %collective-permute-start.19 = (f32[256,1024]{1,0:T(8,128)S(1)}, f32[256,1024]{1,0:T(8,128)S(1)}, u32[]{:S(2)}, u32[]{:S(2)}) collective-permute-start(f32[256,1024]{1,0:T(8,128)S(1)} %collective-permute-done.18.refs_2_), channel_id=1, source_target_pairs={{2,6},{7,3},{8,12},{13,9},{18,22},{23,19},{24,28},{29,25}} | collective-permute-start | bytes 3145736 | tf_op jit(solution)/shard_map/ppermute | solution.py:196
  94.7 19.9 %collective-permute-start.13 = (f32[160,1024]{1,0:T(8,128)S(1)}, f32[160,1024]{1,0:T(8,128)S(1)}, u32[]{:S(2)}, u32[]{:S(2)}) collective-permute-start(f32[160,1024]{1,0:T(8,128)S(1)} %get-tuple-element.19), channel_id=1, source_target_pairs={{0,16},{1,17},{2,18},{3,19},{4,20},{5,21},{6,22},{7,23},{8,24},{9,... | collective-permute-start | bytes 1966088 | tf_op jit(solution)/shard_map/ppermute | solution.py:196
  100.9 16.0 %collective-permute-start.7 = (f32[160,1024]{1,0:T(8,128)S(1)}, f32[160,1024]{1,0:T(8,128)S(1)}, u32[]{:S(2)}, u32[]{:S(2)}) collective-permute-start(f32[160,1024]{1,0:T(8,128)S(1)} %shard_map.29.refs_0_.refs_8_), channel_id=1, source_target_pairs={{0,8},{5,13},{10,2},{15,7},{16,24},{21,29},{26,18},{31,23}} | collective-permute-start | bytes 1966088 | tf_op jit(solution)/shard_map/ppermute | solution.py:196
  102.3 16.7 %copy-start.1 = (f32[256,1024]{1,0:T(8,128)S(1)}, f32[256,1024]{1,0:T(8,128)}, u32[]{:S(2)}) copy-start(f32[256,1024]{1,0:T(8,128)} %refs_4_.1) | copy-start | bytes 3145732
  102.3 16.7 %copy-start.3 = (f32[256,1024]{1,0:T(8,128)S(1)}, f32[256,1024]{1,0:T(8,128)}, u32[]{:S(2)}) copy-start(f32[256,1024]{1,0:T(8,128)} %copy-done.2) | copy-start | bytes 3145732
  114.6 25.3 %collective-permute-start.5 = (f32[160,1024]{1,0:T(8,128)S(1)}, f32[160,1024]{1,0:T(8,128)S(1)}, u32[]{:S(2)}, u32[]{:S(2)}) collective-permute-start(f32[160,1024]{1,0:T(8,128)S(1)} %shard_map.29.refs_0_.refs_8_), channel_id=1, source_target_pairs={{0,4},{5,1},{10,14},{15,11},{16,20},{21,17},{26,30},{31,27}} | collective-permute-start | bytes 1966088 | tf_op jit(solution)/shard_map/ppermute | solution.py:196
  117.0 23.0 %collective-permute-start.14 = (f32[160,1024]{1,0:T(8,128)S(1)}, f32[160,1024]{1,0:T(8,128)S(1)}, u32[]{:S(2)}, u32[]{:S(2)}) collective-permute-start(f32[160,1024]{1,0:T(8,128)S(1)} %collective-permute-done.13.refs_5_.refs_11_), channel_id=1, source_target_pairs={{1,0},{2,3},{5,4},{6,7},{9,8},{10,11},{13,12},{14,15},{17,16},{18,... | collective-permute-start | bytes 1966088 | tf_op jit(solution)/shard_map/ppermute | solution.py:196
  118.3 21.7 %collective-permute-start.9 = (f32[160,1024]{1,0:T(8,128)S(1)}, f32[160,1024]{1,0:T(8,128)S(1)}, u32[]{:S(2)}, u32[]{:S(2)}) collective-permute-start(f32[160,1024]{1,0:T(8,128)S(1)} %collective-permute-done.7.refs_4_), channel_id=1, source_target_pairs={{2,6},{7,3},{8,12},{13,9},{18,22},{23,19},{24,28},{29,25}} | collective-permute-start | bytes 1966088 | tf_op jit(solution)/shard_map/ppermute | solution.py:196
  124.9 15.0 %collective-permute-start.15 = (f32[96,1024]{1,0:T(8,128)S(1)}, f32[96,1024]{1,0:T(8,128)S(1)}, u32[]{:S(2)}, u32[]{:S(2)}) collective-permute-start(f32[96,1024]{1,0:T(8,128)S(1)} %collective-permute-done.4.refs_1_), channel_id=1, source_target_pairs={{0,16},{3,19},{4,20},{7,23},{8,24},{11,27},{12,28},{15,31},{16,0},... | collective-permute-start | bytes 1179656 | tf_op jit(solution)/shard_map/ppermute | solution.py:196
  128.0 12.0 %collective-permute-start.10 = (f32[96,1024]{1,0:T(8,128)S(1)}, f32[96,1024]{1,0:T(8,128)S(1)}, u32[]{:S(2)}, u32[]{:S(2)}) collective-permute-start(f32[96,1024]{1,0:T(8,128)S(1)} %collective-permute-done.8.refs_5_), channel_id=1, source_target_pairs={{2,6},{7,3},{8,12},{13,9},{18,22},{23,19},{24,28},{29,25}} | collective-permute-start | bytes 1179656 | tf_op jit(solution)/shard_map/ppermute | solution.py:196
